TPU v7x, 512 devices: a 8x2x16 block of a 8x16x16 slice. The times are simulated.
512 devices in a mesh: groups: 2 (over y), seq: 16 (over z), head: 8 (over x), rep: 2 (over core).
Axes of the slice: x: 8, y: 2, z: 16, core: 2. Of those that a mesh axis runs over, the one named last changes fastest.
The devices are a block of a 8x16x16 slice.
Arguments:
- kv_cache: bfloat16 [2, 1024, 8, 128, 256], P(None, ('groups', 'seq'), 'head', 'rep'), parts along dimension 1, may hold values from -6 to 6
- keep_list: int32 [4, 256], P('groups'), parts along dimension 0, may hold values from -1 to 511, as said below
- page_slot: int32 [4, 256], P('groups'), parts along dimension 0, may hold values from -1 to 255, as said below
Outputs:
- paged_cache: bfloat16 [2, 512, 8, 128, 256], P(None, ('groups', 'seq'), 'head', 'rep'), parts along dimension 1
- page_bounds: bfloat16 [2, 512, 8, 2, 128], P(None, ('groups', 'seq'), 'head'), parts along dimension 1
There are 2 independent parts, one for each index of `groups`. A program takes and returns all parts, laid end to end along the dimension named above; each array names one. Nothing has to cross between parts.
Inputs may be any that keep to these rules, and one draw needn't show every extreme that they name: `keep_list`: row l holds count_l distinct block indices in rising order, then -1 in the remaining entries. Of one row, at most 16 listed blocks lie on one seq shard (blocks s * 32 to s * 32 + 31); row 0 reaches this on every shard. `page_slot`: entry (l, j) is the page of block keep_list[l, j]: distinct pages for the count_l listed blocks of a row, -1 after them. Of one row, at most 2 blocks of one seq shard go to pages of one owner (pages o * 16 to o * 16 + 15), and this is reached in every draw.
All inputs are finite; a program needn't handle non-finite values.
Results may differ from a plain program's by a relative error of at most 0.001.
Values may be sent and summed in bfloat16 or wider, within the bound.
No kernel may reach another device: no remote copies, remote signals or barrier semaphores. Data moves between devices by JAX's collectives and lax.ppermute only.
A program may use at most 64 MiB of HBM per device.

v0:
```python
import jax
import jax.numpy as jnp
from jax import lax
from jax.sharding import PartitionSpec as P


def gathered_once(array, axis):
    leaves = jax.tree.leaves(array)
    order = sorted(range(len(leaves)), key=lambda k: -leaves[k].size)
    width = (1, *leaves[order[0]].shape)[-1]
    lines = [
        jnp.pad(leaves[k].reshape(-1), (0, -leaves[k].size % width)).reshape(-1, width)
        for k in order
    ]
    both, at, found = (lax.all_gather(jnp.concatenate(lines), axis), 0, {})
    for k, line in zip(order, lines):
        section = both[:, at : at + len(line)].reshape(len(both), -1)
        found[k] = section[:, : leaves[k].size].reshape(-1, *leaves[k].shape)
        at += len(line)
    numbers = iter(range(len(leaves)))
    return jax.tree.map(lambda _: found[next(numbers)], array)


def combined_all(value, axis, join):
    pieces = gathered_once(value, axis)
    head = jax.tree.map(lambda part: part[0], pieces)
    tail = jax.tree.map(lambda part: part[1:], pieces)
    subtotal, _ = lax.scan(lambda subtotal, section: (join(subtotal, section), None), head, tail)
    return subtotal


def pack_slots(block_rows, sent_here, destination, local_block, slot_width):
    blk_dev = block_rows.shape[1]
    slot_hot = (
        destination[:, :, None] == jnp.arange(slot_width, dtype=jnp.int32)[None, None, :]
    ) & sent_here[:, :, None]
    block_hot = local_block[:, :, None] == jnp.arange(blk_dev, dtype=jnp.int32)[None, None, :]
    select = jnp.einsum(
        "ljw,ljb->lwb", slot_hot.astype(jnp.float32), block_hot.astype(jnp.float32)
    ).astype(jnp.bfloat16)
    return jnp.einsum(
        "lwb,lbr->lwr", select, block_rows, preferred_element_type=jnp.float32
    ).astype(jnp.bfloat16)


def place_index(takers, in_page, incoming, page_dev):
    page_hot = (
        in_page[:, :, None] == jnp.arange(page_dev, dtype=jnp.int32)[None, None, :]
    ) & takers[:, :, None]
    return jnp.sum(jnp.where(page_hot, incoming[:, :, None] + 1, 0), axis=1) - 1


def place_pages(target, shard_part):
    width = shard_part.shape[1]
    one_hot = (target[:, :, None] == jnp.arange(width, dtype=jnp.int32)[None, None, :]).astype(
        jnp.bfloat16
    )
    return jnp.einsum("lpn,lnr->lpr", one_hot, shard_part, preferred_element_type=jnp.float32)


def extend(first, second):
    return (jnp.maximum(first[0], second[0]), jnp.minimum(first[1], second[1]))


def on_device(kv_cache, keep_list, page_slot):
    layer_count, page_count = keep_list.shape
    blk_dev = kv_cache.shape[1]
    seq_count = lax.axis_size("seq")
    page_dev = page_count // seq_count
    capacity = (page_dev - 2) // seq_count + 2
    seq_index = lax.axis_index("seq")
    block_rows = kv_cache.reshape(layer_count, blk_dev, -1)
    position = jnp.arange(page_count, dtype=jnp.int32)
    counts = jnp.array(
        [page_count - layer * page_count // (2 * layer_count) for layer in range(layer_count)],
        jnp.int32,
    )
    listed = position[None, :] < counts[:, None]
    source = keep_list // blk_dev
    local_block = keep_list % blk_dev
    owner_index = page_slot // page_dev
    in_page = page_slot % page_dev
    earlier = (position[None, None, :] < position[None, :, None]) & listed[:, None, :]
    same_source = source[:, :, None] == source[:, None, :]
    sent_here = listed & (source == seq_index)
    takers = listed & (owner_index == seq_index)
    same_owner = owner_index[:, :, None] == owner_index[:, None, :]
    slot_rank = jnp.sum(earlier & same_source & same_owner, axis=2)
    packed = pack_slots(
        block_rows, sent_here, owner_index * capacity + slot_rank, local_block, seq_count * capacity
    )
    received = lax.all_to_all(packed, "seq", split_axis=1, concat_axis=1, tiled=True)
    target = place_index(takers, in_page, source * capacity + slot_rank, page_dev)
    gathered = place_pages(target, received)
    paged_cache = gathered.astype(jnp.bfloat16).reshape(
        (layer_count, page_dev) + kv_cache.shape[2:]
    )
    head_width = kv_cache.shape[-1] // 2
    key_part = paged_cache[..., :head_width]
    key_high = jnp.max(key_part, axis=3)
    key_low = jnp.min(key_part, axis=3)
    upper_bound, lower_bound = combined_all((key_high, key_low), "rep", extend)
    page_bounds = jnp.stack([upper_bound, lower_bound], axis=3)
    return (paged_cache, page_bounds)


def solution(mesh):
    in_specs = (
        P(None, ("groups", "seq"), "head", "rep", None),
        P("groups", None),
        P("groups", None),
    )
    out_specs = (
        P(None, ("groups", "seq"), "head", "rep", None),
        P(None, ("groups", "seq"), "head", None, None),
    )
    return jax.shard_map(
        on_device, mesh=mesh, in_specs=in_specs, out_specs=out_specs, check_vma=False
    )
```

profile of v0, /device:TPU:65, one launch (start us, length us, event | category | flops | bytes accessed | tf_op | source)
XLA Modules:
  0.0 158.4 jit_solution(9617120926331949293)
XLA Ops:
  0.7 0.8 compare_and_fusion
  1.5 0.3 convert_reduce_fusion
  1.8 0.7 add_add_fusion
  2.5 4.2 %reshape.123 = bf16[2,32,16384]{2,1,0:T(8,128)(2,1)} reshape(bf16[2,32,1,64,256]{4,3,2,1,0:T(8,128)(2,1)} %param.4) | data formatting | bytes 4194304 | tf_op jit(solution)/shard_map/reshape | solution.py:72
  6.7 2.4 %convolution_convert_fusion = bf16[2,32,16384]{2,1,0:T(8,128)(2,1)S(1)} fusion(bf16[2,32,16384]{2,1,0:T(8,128)(2,1)} %reshape.123, s32[2,256]{1,0:T(2,128)S(1)} %get-tuple-element.39, s32[2,256]{1,0:T(2,128)S(1)} %get-tuple-element.34, pred[2,256]{1,0:T(4,128)(4,1)S(1)} %get-tuple-element.29), kind=kOutput, calls=%fused_computation | convolution fusion | flops 69257216 | bytes 4198912 | tf_op jit(solution)/shard_map/lwb,lbr->lwr/dot_general | solution.py:41
  9.1 3.5 %copy.13 = bf16[2,32,16384]{2,0,1:T(2,128)(2,1)} copy(bf16[2,32,16384]{2,1,0:T(8,128)(2,1)S(1)} %convolution_convert_fusion) | data formatting | bytes 4194304 | tf_op jit(solution)/shard_map/convert_element_type | solution.py:43
  12.6 0.0 copy-start.1
  12.6 44.3 %all-to-all-start = ((bf16[2,32,16384]{2,0,1:T(2,128)(2,1)}), bf16[2,32,16384]{2,0,1:T(2,128)(2,1)S(1)}, u32[]{:S(2)}, u32[]{:S(2)}) async-start(bf16[2,32,16384]{2,0,1:T(2,128)(2,1)} %copy.13), calls=%async_computation | async-start | bytes 4194304 | tf_op jit(solution)/shard_map/all_to_all | solution.py:92
  57.0 0.0 copy-done.1
  57.0 0.1 select_reduce_fusion
  57.1 91.5 %all-to-all-done = bf16[2,32,16384]{2,0,1:T(2,128)(2,1)S(1)} async-done(((bf16[2,32,16384]{2,0,1:T(2,128)(2,1)}), bf16[2,32,16384]{2,0,1:T(2,128)(2,1)S(1)}, u32[]{:S(2)}, u32[]{:S(2)}) %all-to-all-start) | async-done | bytes 2097184 | tf_op jit(solution)/shard_map/all_to_all | solution.py:92
  148.7 2.3 %convolution_convert_fusion.1 = bf16[2,16,16384]{2,1,0:T(8,128)(2,1)S(1)} fusion(bf16[2,32,16384]{2,0,1:T(2,128)(2,1)S(1)} %all-to-all-done, s32[2,16]{1,0:T(2,128)S(1)} %broadcast_add_fusion), kind=kOutput, calls=%fused_computation.1 | convolution fusion | flops 34079744 | bytes 3145856 | tf_op jit(solution)/shard_map/lpn,lnr->lpr/dot_general | solution.py:58
  151.0 0.2 copy.17
  151.3 0.0 copy-start
  151.3 0.2 slice_reduce_fusion.1
  151.5 6.3 %all-gather = bf16[128,128]{1,0:T(8,128)(2,1)S(1)} all-gather(bf16[64,128]{1,0:T(8,128)(2,1)S(1)} %pad_maximum_fusion), channel_id=2, replica_groups=mesh['groups'=2,'seq'=16,'head'=8,'rep'=2] {'rep'}, dimensions={0}, use_global_device_ids=true | all-gather | bytes 49152 | tf_op jit(solution)/shard_map/all_gather | solution.py:15
  157.8 0.6 copy.16
  158.4 0.0 copy-done
  (6 shorter events, 0.1 us)
Async XLA Ops:
  12.6 44.4 %copy-start.1 = (s32[2,256]{1,0:T(2,128)S(1)}, s32[2,256]{1,0:T(2,128)}, u32[]{:S(2)}) copy-start(s32[2,256]{1,0:T(2,128)} %param.6) | copy-start | bytes 6148
  12.6 136.1 %all-to-all-start = ((bf16[2,32,16384]{2,0,1:T(2,128)(2,1)}), bf16[2,32,16384]{2,0,1:T(2,128)(2,1)S(1)}, u32[]{:S(2)}, u32[]{:S(2)}) async-start(bf16[2,32,16384]{2,0,1:T(2,128)(2,1)} %copy.13), calls=%async_computation | async-start | bytes 4194304 | tf_op jit(solution)/shard_map/all_to_all | solution.py:92
  151.3 7.2 %copy-start = (bf16[4,8,64,256]{3,2,1,0:T(8,128)(2,1)}, bf16[4,8,64,256]{3,2,1,0:T(8,128)(2,1)S(1)}, u32[]{:S(2)}) copy-start(bf16[4,8,64,256]{3,2,1,0:T(8,128)(2,1)S(1)} %copy.17) | copy-start | bytes 3145732
where the time goes:
time: 159 us; the launch traced here: 158 us
  waiting for transfers between devices  91.5 us (58%)
  starting transfers between devices  44.3 us (28%)
  local copies, waits for them, and re-layouts  8.59 us (5%)
  blocking collectives  6.3 us (4%)
  matrix products  4.75 us (3%)
  other arithmetic  2.19 us (1%)
    all_to_all x1, waiting for transfers between devices, on_device(): lax.all_to_all(packed, 'seq', split_axis=1, concat_axis=1, tiled=True)  91.5 us
    all_to_all x1, starting transfers between devices, on_device(): lax.all_to_all(packed, 'seq', split_axis=1, concat_axis=1, tiled=True)  44.3 us
    all_gather x1, blocking collectives, gathered_once(): both, at, found = (lax.all_gather(jnp.concatenate(lines), axis), 0, {})  6.3 us
    reshape x1, local copies, waits for them, and re-layouts, on_device(): block_rows = kv_cache.reshape(layer_count, blk_dev, -1)  4.21 us
    convert_element_type x1, local copies, waits for them, and re-layouts, pack_slots(): return jnp.einsum('lwb,lbr->lwr', select, block_rows, preferred_element_t...  3.51 us
  transfers between devices with their start and end apart: 1, of which 1 were waited for; matrix products, arithmetic and copies ran while one was open for 0% of the time, Pallas kernels for 0%

commit v1 on v0

v1 whole, which is shorter than its diff:
```python
import functools

import jax
import jax.numpy as jnp
from jax import lax
from jax.experimental import pallas as pl
from jax.experimental.pallas import tpu as pltpu
from jax.sharding import PartitionSpec as P


def copy_through(fetches, out_ref, stage, sem_in, sem_out):
    into = [
        pltpu.make_async_copy(source, stage.at[k], sem_in.at[k])
        for k, source in enumerate(fetches)
    ]
    back = [
        pltpu.make_async_copy(stage.at[k], out_ref.at[k], sem_out.at[k])
        for k in range(len(fetches))
    ]
    for copy in into:
        copy.start()
    for arrive, leave in zip(into, back):
        arrive.wait()
        leave.start()
    for copy in back:
        copy.wait()


def pack_kernel(index_ref, cache_ref, out_ref, stage, sem_in, sem_out):
    layers, owners = index_ref.shape
    fetches = [
        cache_ref.at[layer, index_ref[layer, owner], 0]
        for owner in range(owners)
        for layer in range(layers)
    ]
    copy_through(fetches, out_ref, stage, sem_in, sem_out)


def pick_kernel(index_ref, layer_ref, cache_ref, out_ref, stage, sem_in, sem_out):
    fetches = [cache_ref.at[layer_ref[k], index_ref[k], 0] for k in range(index_ref.shape[0])]
    copy_through(fetches, out_ref, stage, sem_in, sem_out)


def gather_blocks(kernel, scalars, cache, count):
    block = cache.shape[3:]
    return pl.pallas_call(
        kernel,
        grid_spec=pltpu.PrefetchScalarGridSpec(
            num_scalar_prefetch=len(scalars),
            grid=(1,),
            in_specs=[pl.BlockSpec(memory_space=pltpu.HBM)],
            out_specs=pl.BlockSpec(memory_space=pltpu.HBM),
            scratch_shapes=[
                pltpu.VMEM((count, *block), cache.dtype),
                pltpu.SemaphoreType.DMA((count,)),
                pltpu.SemaphoreType.DMA((count,)),
            ],
        ),
        out_shape=jax.ShapeDtypeStruct((count, *block), cache.dtype),
        compiler_params=pltpu.CompilerParams(vmem_limit_bytes=8 << 20),
    )(*scalars, cache)


def place_kernel(
    table_ref, many_ref, base_ref, left_ref, right_ref, extra_ref,
    out_ref, bounds_ref, empty, spare, rows, sem, spare_sem,
):
    pages, slots = out_ref.shape[0], base_ref.shape[0]
    head_width = base_ref.shape[-1] // 2
    empty[...] = jnp.zeros_like(empty)

    @pl.when(many_ref[0] != 0)
    def _():
        copy = pltpu.make_async_copy(extra_ref, spare, spare_sem)
        copy.start()
        copy.wait()

    def put(i, ref):
        pltpu.make_async_copy(ref, out_ref.at[i], sem.at[i]).start()
        keys = ref[:, :head_width].astype(jnp.float32)
        rows[pl.ds(2 * i, 1), :] = jnp.max(keys, axis=0, keepdims=True)
        rows[pl.ds(2 * i + 1, 1), :] = -jnp.min(keys, axis=0, keepdims=True)

    for i in range(pages):
        t = table_ref[i // table_ref.shape[1], i % table_ref.shape[1]]

        @pl.when(t < 0)
        def _():
            pltpu.make_async_copy(empty, out_ref.at[i], sem.at[i]).start()
            rows[pl.ds(2 * i, 2), :] = jnp.zeros((2, head_width), jnp.float32)

        @pl.when((t >= 0) & (t < slots))
        def _():
            put(i, base_ref.at[jnp.clip(t, 0, slots - 1)])

        @pl.when(t == slots)
        def _():
            put(i, left_ref)

        @pl.when(t == slots + 1)
        def _():
            put(i, right_ref)

        @pl.when(t >= slots + 2)
        def _():
            put(i, spare.at[jnp.clip(t - slots - 2, 0, slots - 1)])

    bounds_ref[...] = rows[...].astype(bounds_ref.dtype)
    for i in range(pages):
        pltpu.make_async_copy(empty, out_ref.at[i], sem.at[i]).wait()


def place_pages(table, many, base, left, right, extra, pages):
    block, head_width = base.shape[1:], base.shape[-1] // 2
    vmem = pl.BlockSpec(memory_space=pltpu.VMEM)
    hbm = pl.BlockSpec(memory_space=pltpu.HBM)
    return pl.pallas_call(
        place_kernel,
        grid_spec=pltpu.PrefetchScalarGridSpec(
            num_scalar_prefetch=2,
            grid=(1,),
            in_specs=[vmem, vmem, vmem, hbm],
            out_specs=[hbm, vmem],
            scratch_shapes=[
                pltpu.VMEM(block, base.dtype),
                pltpu.VMEM(base.shape, base.dtype),
                pltpu.VMEM((2 * pages, head_width), jnp.float32),
                pltpu.SemaphoreType.DMA((pages,)),
                pltpu.SemaphoreType.DMA,
            ],
        ),
        out_shape=[
            jax.ShapeDtypeStruct((pages, *block), base.dtype),
            jax.ShapeDtypeStruct((2 * pages, head_width), base.dtype),
        ],
        compiler_params=pltpu.CompilerParams(vmem_limit_bytes=8 << 20),
    )(table, many, base, left, right, extra)


def swap(block, shift, size):
    if shift == 0:
        return block
    return lax.ppermute(block, "seq", [(s, (s + shift) % size) for s in range(size)])


def on_device(kv_cache, keep_list, page_slot):
    layer_count, page_count = keep_list.shape
    blk_dev = kv_cache.shape[1]
    seq_count = lax.axis_size("seq")
    rep_count = lax.axis_size("rep")
    page_dev = page_count // seq_count
    slots = seq_count * layer_count
    me = lax.axis_index("seq")
    shards = jnp.arange(seq_count, dtype=jnp.int32)

    my_block = me * blk_dev
    my_page = shards * page_dev
    sent = (keep_list >= my_block) & (keep_list < my_block + blk_dev)
    owned = (page_slot[:, None, :] >= my_page[None, :, None]) & (
        page_slot[:, None, :] < my_page[None, :, None] + page_dev
    )
    local = jnp.where(sent, keep_list - my_block, -1)[:, None, :]
    first = jnp.min(jnp.where(owned & (local >= 0), local, blk_dev), axis=2)
    first = jnp.where(first == blk_dev, 0, first)
    payload = gather_blocks(pack_kernel, (first,), kv_cache, slots)

    def exchange(blocks):
        shaped = blocks.reshape(seq_count, layer_count, *blocks.shape[1:])
        moved = lax.all_to_all(shaped, "seq", split_axis=0, concat_axis=0, tiled=True)
        return moved.reshape(blocks.shape)

    base = exchange(payload)
    keep_list, page_slot, payload = lax.optimization_barrier((keep_list, page_slot, payload))

    def split(count):
        return count.bit_length() - 1

    source, owner = keep_list >> split(blk_dev), page_slot >> split(page_dev)
    local = jnp.where(source == me, keep_list - me * blk_dev, 0)[:, None, :]
    second = jnp.max(jnp.where(owner[:, None, :] == shards[None, :, None], local, 0), axis=2)
    position = jnp.arange(page_count, dtype=jnp.int32)
    pair = jnp.where(keep_list >= 0, source * seq_count + owner, -1 - position)
    again = jnp.any(
        (pair[:, :, None] == pair[:, None, :]) & (position[None, :] < position[:, None])[None], axis=2
    )
    shift = jnp.where(owner >= source, owner - source, owner - source + seq_count)
    active = jnp.any(again[:, None, :] & (shift[:, None, :] == shards[None, :, None]), axis=2)
    number = jnp.arange(slots, dtype=jnp.int32).reshape(layer_count, seq_count)
    none = jnp.int32(2 * slots)
    class_a = jnp.min(jnp.where(active, number, none))
    class_b = jnp.min(jnp.where(active & (number > class_a), number, none))
    many = jnp.any(active & (number > class_b)).astype(jnp.int32)
    shift_a = jnp.where(class_a < none, lax.rem(class_a, seq_count), 0)
    shift_b = jnp.where(class_b < none, lax.rem(class_b, seq_count), 0)
    flip = shift_a > shift_b
    class_a, class_b = jnp.where(flip, class_b, class_a), jnp.where(flip, class_a, class_b)
    shift_a, shift_b = jnp.where(flip, shift_b, shift_a), jnp.where(flip, shift_a, shift_b)
    classes = jnp.stack([class_a, class_b])
    shifts = jnp.stack([shift_a, shift_b])
    class_layer = jnp.where(classes < none, lax.div(classes, seq_count), 0)
    wanted = class_layer * seq_count + lax.rem(me + shifts, seq_count)
    wanted = wanted[:, None, None] == number[None]
    class_block = jnp.sum(jnp.where(wanted, second[None], 0), axis=(1, 2))
    pair_blocks = gather_blocks(pick_kernel, (class_block, class_layer), kv_cache, 2)

    page = me * page_dev + jnp.arange(page_dev, dtype=jnp.int32)
    held = jnp.max(
        jnp.where(page_slot[:, None, :] == page[None, :, None], keep_list[:, None, :], -1), axis=2
    )
    origin = held >> split(blk_dev)
    later = jnp.any(
        (origin[:, :, None] == origin[:, None, :]) & (held[:, None, :] < held[:, :, None]), axis=2
    )
    layers = jnp.arange(layer_count, dtype=jnp.int32)[:, None]
    slot = origin * layer_count + layers
    back = jnp.where(me >= origin, me - origin, me - origin + seq_count)
    moved_slot = jnp.where(layers * seq_count + back == class_a, slots, slots + 1)
    table = jnp.where(later, jnp.where(many > 0, slots + 2 + slot, moved_slot), slot)
    table = jnp.where(held < 0, -1, table).astype(jnp.int32)

    branches = [
        lambda one, two, one_by=a, two_by=b: (
            swap(one, one_by, seq_count),
            swap(two, two_by, seq_count),
        )
        for b in range(seq_count)
        for a in range(b + 1)
    ]
    branch = shift_b * (shift_b + 1) // 2 + shift_a
    branch, pair_blocks, table = lax.optimization_barrier((branch, pair_blocks, table))
    left, right = lax.switch(branch, branches, pair_blocks[0], pair_blocks[1])

    def all_seconds(state):
        rounds, index, _ = lax.optimization_barrier(state)
        return rounds - 1, index, exchange(gather_blocks(pack_kernel, (index,), kv_cache, slots))

    base, payload, many = lax.optimization_barrier((base, payload, many))
    _, _, extra = lax.while_loop(lambda state: state[0] > 0, all_seconds, (many, second, payload))

    pages, half = place_pages(
        table, many.reshape(1), base, left, right, extra, layer_count * page_dev
    )
    other = lax.ppermute(half, "rep", [(r, (r + 1) % rep_count) for r in range(rep_count)])
    width = half.shape[-1]
    high = jnp.maximum(half, other).reshape(layer_count, page_dev, 1, 2, width)
    is_low = lax.broadcasted_iota(jnp.int32, high.shape, 3) == 1
    page_bounds = jnp.where(is_low, -high, high)
    paged_cache = pages.reshape(layer_count, page_dev, *kv_cache.shape[2:])
    return paged_cache, page_bounds


def solution(mesh):
    in_specs = (
        P(None, ("groups", "seq"), "head", "rep", None),
        P("groups", None),
        P("groups", None),
    )
    out_specs = (
        P(None, ("groups", "seq"), "head", "rep", None),
        P(None, ("groups", "seq"), "head", None, None),
    )
    return jax.shard_map(
        on_device, mesh=mesh, in_specs=in_specs, out_specs=out_specs, check_vma=False
    )
```

time: 159 us -> 114 us (0.72)
  the two profiles are of different devices: /device:TPU:65 before, /device:TPU:85 now
where the time goes in v1:
time: 114 us
  starting transfers between devices  64.4 us (56%)
  waiting for transfers between devices  26.8 us (24%)
  between operations  9.31 us (8%)
  other arithmetic  6.75 us (6%)
  Pallas kernels  6.49 us (6%)
    all_to_all x1, starting transfers between devices, exchange(): lax.all_to_all(shaped, 'seq', split_axis=0, concat_axis=0, tiled=True)  43.4 us
    ppermute x2, waiting for transfers between devices, swap(): lax.ppermute(block, 'seq', [(s, (s + shift) % size) for s in range(size)])  26 us
    ppermute x2, starting transfers between devices, swap(): lax.ppermute(block, 'seq', [(s, (s + shift) % size) for s in range(size)])  14 us
    ppermute x1, starting transfers between devices, on_device(): lax.ppermute(half, 'rep', [(r, (r + 1) % rep_count) for r in range(rep_co...  6.97 us
    pallas_call x2, Pallas kernels, gather_blocks(): pl.pallas_call(kernel, grid_spec=pltpu.PrefetchScalarGridSpec(num_scalar_...  3.77 us
    pallas_call x1, Pallas kernels, place_pages(): pl.pallas_call(place_kernel, grid_spec=pltpu.PrefetchScalarGridSpec(num_s...  2.72 us
  transfers between devices with their start and end apart: 4, of which 3 were waited for; matrix products, arithmetic and copies ran while one was open for 4% of the time, Pallas kernels for 1%

profile of v1, /device:TPU:85, one launch (start us, length us, event | category | flops | bytes accessed | tf_op | source)
XLA Modules:
  0.0 113.9 jit_solution(3742009585541479237)
XLA Ops:
  0.7 0.7 broadcast_compare_fusion
  1.3 0.9 select_reduce_fusion.2
  2.2 0.0 copy-start.1
  2.2 0.0 copy-start.2
  2.2 0.0 copy-start
  2.3 3.0 %shard_map.50 = bf16[32,64,256]{2,1,0:T(8,128)(2,1)} custom-call(s32[2,16]{1,0:T(2,128)S(1)} %compare_select_fusion.4.index_ref, bf16[2,32,1,64,256]{4,3,2,1,0:T(8,128)(2,1)} %cache_ref.3), custom_call_target="tpu_custom_call" | custom-call | tf_op jit(solution)/shard_map/pallas_call | solution.py:46
  5.3 43.4 %all-to-all-start.1 = ((bf16[16,2,64,256]{3,2,1,0:T(8,128)(2,1)}), bf16[16,2,64,256]{3,2,1,0:T(8,128)(2,1)S(1)}, u32[]{:S(2)}, u32[]{:S(2)}) async-start(bf16[16,2,64,256]{3,2,1,0:T(8,128)(2,1)} %bitcast.6), calls=%async_computation.1 | async-start | bytes 2097152 | tf_op jit(solution)/shard_map/all_to_all | solution.py:169
  48.7 0.0 copy-done.1
  48.8 0.0 copy-done.2
  48.8 0.3 and_reduce_fusion
  49.0 0.1 fusion.1
  49.2 0.6 select_reduce_fusion.3
  49.8 1.3 %fusion.3 = s32[]{:T(128)} fusion(pred[2,16]{1,0:T(4,128)(4,1)S(1)} %fusion.1, s32[]{:T(128)} %select_reduce_fusion.3), kind=kLoop, calls=%fused_computation.30 | loop fusion | flops 191 | bytes 40 | tf_op jit(solution)/shard_map/reduce_min | solution.py:191
  58.9 1.3 %and_reduce_fusion.2 = pred[]{:T(512)} fusion(pred[2,16]{1,0:T(4,128)(4,1)S(1)} %fusion.1, s32[]{:T(128)} %fusion.3), kind=kLoop, calls=%fused_computation.26 | loop fusion | flops 159 | bytes 37 | tf_op jit(solution)/shard_map/reduce_or | solution.py:192
  60.8 0.1 fusion.9
  60.9 0.1 select_reduce_fusion.1
  61.0 0.2 fusion.2.index_ref
  61.2 0.0 copy-done
  61.3 0.8 shard_map.51
  62.0 0.2 select_reduce_fusion
  62.2 0.2 and_reduce_fusion.1
  62.4 0.1 compare_select_fusion.11.table_ref
  62.5 40.1 %conditional.1 = ((bf16[64,256]{1,0:T(8,128)(2,1)S(1)}, bf16[64,256]{1,0:T(8,128)(2,1)S(1)})) conditional(s32[]{:T(128)} %clamp.3, (bf16[64,256]{1,0:T(8,128)(2,1)S(1)}, bf16[64,256]{1,0:T(8,128)(2,1)S(1)}) %tuple.574, (bf16[64,256]{1,0:T(8,128)(2,1)S(1)}, bf16[64,256]{1,0:T(8,128)(2,1)S(1)}) %slice_bitcast_fusion, ...), branch_computations={%region_10.11_spmd, %region_11.12_spmd, %region_12.13_spmd, %regio... | conditional | bytes 393320 | solution.py:231
  62.6 3.1 %collective-permute-start.49 = (bf16[64,256]{1,0:T(8,128)(2,1)S(1)}, bf16[64,256]{1,0:T(8,128)(2,1)S(1)}, u32[]{:S(2)}, u32[]{:S(2)}) collective-permute-start(bf16[64,256]{1,0:T(8,128)(2,1)S(1)} %get-tuple-element.645), channel_id=1, source_target_pairs={{0,16},{16,32},{32,48},{48,64},{64,80},{80,96},{96,112},{112,128},... | collective-permute-start | bytes 98312 | tf_op jit(solution)/shard_map/cond/branch_29_fun/ppermute | solution.py:143
  65.7 10.9 %collective-permute-start.50 = (bf16[64,256]{1,0:T(8,128)(2,1)S(1)}, bf16[64,256]{1,0:T(8,128)(2,1)S(1)}, u32[]{:S(2)}, u32[]{:S(2)}) collective-permute-start(bf16[64,256]{1,0:T(8,128)(2,1)S(1)} %get-tuple-element.646), channel_id=1, source_target_pairs={{0,112},{16,128},{32,144},{48,160},{64,176},{80,192},{96,208},{112... | collective-permute-start | bytes 98312 | tf_op jit(solution)/shard_map/cond/branch_29_fun/ppermute | solution.py:143
  76.6 19.6 %collective-permute-done.49 = bf16[64,256]{1,0:T(8,128)(2,1)S(1)} collective-permute-done((bf16[64,256]{1,0:T(8,128)(2,1)S(1)}, bf16[64,256]{1,0:T(8,128)(2,1)S(1)}, u32[]{:S(2)}, u32[]{:S(2)}) %collective-permute-start.49) | collective-permute-done | bytes 32800 | tf_op jit(solution)/shard_map/cond/branch_29_fun/ppermute | solution.py:143
  96.2 6.4 %collective-permute-done.50 = bf16[64,256]{1,0:T(8,128)(2,1)S(1)} collective-permute-done((bf16[64,256]{1,0:T(8,128)(2,1)S(1)}, bf16[64,256]{1,0:T(8,128)(2,1)S(1)}, u32[]{:S(2)}, u32[]{:S(2)}) %collective-permute-start.50) | collective-permute-done | bytes 32800 | tf_op jit(solution)/shard_map/cond/branch_29_fun/ppermute | solution.py:143
  102.6 0.0 all-to-all-done.1
  102.6 2.7 %shard_map.52 = (bf16[32,64,256]{2,1,0:T(8,128)(2,1)}, bf16[64,128]{1,0:T(8,128)(2,1)S(1)}) custom-call(s32[2,16]{1,0:T(2,128)S(1)} %compare_select_fusion.11.table_ref, s32[1]{0:T(128)} %bitcast.8.many_ref, bf16[32,64,256]{2,1,0:T(8,128)(2,1)S(1)} %bitcast.23, bf16[64,256]{1,0:T(8,128)(2,1)S(1)} %get-tuple-element.889.left_ref, ...), custom_call_target="tpu_custom_call" | custom-call | tf_op jit(solution)/shard_map/pallas_call | solution.py:117
  105.4 7.0 %collective-permute-start.255 = (bf16[64,128]{1,0:T(8,128)(2,1)S(1)}, bf16[64,128]{1,0:T(8,128)(2,1)S(1)}, u32[]{:S(2)}, u32[]{:S(2)}) collective-permute-start(bf16[64,128]{1,0:T(8,128)(2,1)S(1)} %get-tuple-element.894), channel_id=1, source_target_pairs={{0,1},{1,0},{2,3},{3,2},{4,5},{5,4},{6,7},{7,6},{8,9},{9,8},{10,11... | collective-permute-start | bytes 49160 | tf_op jit(solution)/shard_map/ppermute | solution.py:243
  112.4 0.8 collective-permute-done.255
  113.2 0.7 broadcast_select_fusion
  (15 shorter events, 0.1 us)
Async XLA Ops:
  2.2 46.5 %copy-start.1 = (s32[2,256]{1,0:T(2,128)S(1)}, s32[2,256]{1,0:T(2,128)}, u32[]{:S(2)}) copy-start(s32[2,256]{1,0:T(2,128)} %param.142) | copy-start | bytes 6148
  2.2 46.5 %copy-start.2 = (s32[2,256]{1,0:T(2,128)S(1)}, s32[2,256]{1,0:T(2,128)}, u32[]{:S(2)}) copy-start(s32[2,256]{1,0:T(2,128)} %param.143) | copy-start | bytes 6148
  2.2 59.0 %copy-start = (bf16[2,32,1,64,256]{4,3,2,1,0:T(8,128)(2,1)S(1)}, bf16[2,32,1,64,256]{4,3,2,1,0:T(8,128)(2,1)}, u32[]{:S(2)}) copy-start(bf16[2,32,1,64,256]{4,3,2,1,0:T(8,128)(2,1)} %cache_ref.3) | copy-start | bytes 6291460
  5.3 97.3 %all-to-all-start.1 = ((bf16[16,2,64,256]{3,2,1,0:T(8,128)(2,1)}), bf16[16,2,64,256]{3,2,1,0:T(8,128)(2,1)S(1)}, u32[]{:S(2)}, u32[]{:S(2)}) async-start(bf16[16,2,64,256]{3,2,1,0:T(8,128)(2,1)} %bitcast.6), calls=%async_computation.1 | async-start | bytes 2097152 | tf_op jit(solution)/shard_map/all_to_all | solution.py:169
  62.6 33.6 %collective-permute-start.49 = (bf16[64,256]{1,0:T(8,128)(2,1)S(1)}, bf16[64,256]{1,0:T(8,128)(2,1)S(1)}, u32[]{:S(2)}, u32[]{:S(2)}) collective-permute-start(bf16[64,256]{1,0:T(8,128)(2,1)S(1)} %get-tuple-element.645), channel_id=1, source_target_pairs={{0,16},{16,32},{32,48},{48,64},{64,80},{80,96},{96,112},{112,128},... | collective-permute-start | bytes 98312 | tf_op jit(solution)/shard_map/cond/branch_29_fun/ppermute | solution.py:143
  65.7 36.9 %collective-permute-start.50 = (bf16[64,256]{1,0:T(8,128)(2,1)S(1)}, bf16[64,256]{1,0:T(8,128)(2,1)S(1)}, u32[]{:S(2)}, u32[]{:S(2)}) collective-permute-start(bf16[64,256]{1,0:T(8,128)(2,1)S(1)} %get-tuple-element.646), channel_id=1, source_target_pairs={{0,112},{16,128},{32,144},{48,160},{64,176},{80,192},{96,208},{112... | collective-permute-start | bytes 98312 | tf_op jit(solution)/shard_map/cond/branch_29_fun/ppermute | solution.py:143
  105.4 7.8 %collective-permute-start.255 = (bf16[64,128]{1,0:T(8,128)(2,1)S(1)}, bf16[64,128]{1,0:T(8,128)(2,1)S(1)}, u32[]{:S(2)}, u32[]{:S(2)}) collective-permute-start(bf16[64,128]{1,0:T(8,128)(2,1)S(1)} %get-tuple-element.894), channel_id=1, source_target_pairs={{0,1},{1,0},{2,3},{3,2},{4,5},{5,4},{6,7},{7,6},{8,9},{9,8},{10,11... | collective-permute-start | bytes 49160 | tf_op jit(solution)/shard_map/ppermute | solution.py:243

commit v2 on v1

v2 whole, which is shorter than its diff:
```python
import functools

import jax
import jax.numpy as jnp
from jax import lax
from jax.experimental import pallas as pl
from jax.experimental.pallas import tpu as pltpu
from jax.sharding import PartitionSpec as P


def forward(fetches, leaves):
    for arrive, leave in zip(fetches, leaves):
        arrive.wait()
        leave.start()
    for leave in leaves:
        leave.wait()


def pack_kernel(index_ref, cache_ref, out_ref, stage, sem_in, sem_out):
    layers, owners = index_ref.shape
    keys = [(layer, owner) for owner in range(owners) for layer in range(layers)]
    fetches = [
        pltpu.make_async_copy(
            cache_ref.at[layer, index_ref[layer, owner], 0], stage.at[k], sem_in.at[k]
        )
        for k, (layer, owner) in enumerate(keys)
    ]
    leaves = [
        pltpu.make_async_copy(stage.at[k], out_ref.at[k], sem_out.at[k]) for k in range(len(keys))
    ]
    for copy in fetches:
        copy.start()
    forward(fetches, leaves)


def pack_seconds(index, cache, count):
    block = cache.shape[3:]
    return pl.pallas_call(
        pack_kernel,
        grid_spec=pltpu.PrefetchScalarGridSpec(
            num_scalar_prefetch=1,
            grid=(1,),
            in_specs=[pl.BlockSpec(memory_space=pltpu.HBM)],
            out_specs=pl.BlockSpec(memory_space=pltpu.HBM),
            scratch_shapes=[
                pltpu.VMEM((count, *block), cache.dtype),
                pltpu.SemaphoreType.DMA((count,)),
                pltpu.SemaphoreType.DMA((count,)),
            ],
        ),
        out_shape=jax.ShapeDtypeStruct((count, *block), cache.dtype),
        compiler_params=pltpu.CompilerParams(vmem_limit_bytes=8 << 20),
    )(index, cache)


def plan_kernel(
    owners, blk_dev, page_dev,
    keep_ref, slot_ref, cache_ref,
    payload_ref, left_ref, right_ref, table_ref, second_ref, choice_ref,
    stage, lists, held_lists, sem_in, sem_out, sem_list,
):
    layers, entries = keep_ref.shape
    slots, none = owners * layers, 2 * owners * layers
    late = 8 * slots
    me = lax.axis_index("seq")
    block_bits, page_bits = blk_dev.bit_length() - 1, page_dev.bit_length() - 1

    row = lax.broadcasted_iota(jnp.int32, (owners, entries), 0)
    square_row = lax.broadcasted_iota(jnp.int32, (owners, owners), 0)
    square_lane = lax.broadcasted_iota(jnp.int32, (owners, owners), 1)
    lane = lax.broadcasted_iota(jnp.int32, (owners, lists.shape[1]), 1)

    def most(values):
        return jnp.max(values.astype(jnp.float32), axis=1, keepdims=True).astype(jnp.int32)

    tables = jnp.zeros(lists.shape, jnp.int32)
    for layer in range(layers):
        keep, slot = keep_ref[pl.ds(layer, 1), :], slot_ref[pl.ds(layer, 1), :]
        source, owner = keep >> block_bits, slot >> page_bits
        chosen = (owner == row) & (source == me)
        local = keep - me * blk_dev
        first = blk_dev - 1 - most(jnp.where(chosen, blk_dev - 1 - local, 0))
        second = most(jnp.where(chosen, local, 0))
        gap = owner - source
        gap = jnp.where(gap < 0, gap + owners, gap)
        by_gap = jnp.where((gap == row) & (keep >= 0), 1.0, 0.0).astype(jnp.bfloat16)
        by_source = jnp.where(source == row, 1.0, 0.0).astype(jnp.bfloat16)
        count = lax.dot_general(
            by_gap, by_source, (((1,), (1,)), ((), ())), preferred_element_type=jnp.float32
        )
        active = (jnp.max(count, axis=1, keepdims=True) > 1.5).astype(jnp.int32)
        held = most(jnp.where(slot == me * page_dev + row, keep, -1))
        across = jnp.max(
            jnp.where(square_row == square_lane, held, -1).astype(jnp.float32), axis=0, keepdims=True
        ).astype(jnp.int32)
        origin = held >> block_bits
        again = most(jnp.where((across >> block_bits == origin) & (across < held), 1, 0))
        found = jnp.where(held < 0, -1, origin * layers + layer + again * late)
        for kind, values in enumerate((first, second, active, found)):
            tables = jnp.where(lane == kind * layers + layer, values, tables)
    lists[...] = tables
    copy = pltpu.make_async_copy(lists, held_lists, sem_list)
    copy.start()
    copy.wait()

    def listed(kind, layer, index):
        return held_lists[index, kind * layers + layer]

    def fetch(layer, index, k):
        return pltpu.make_async_copy(cache_ref.at[layer, index, 0], stage.at[k], sem_in.at[k])

    fetches = []
    for owner in range(owners):
        for layer in range(layers):
            fetches.append(fetch(layer, listed(0, layer, owner), len(fetches)))
            fetches[-1].start()

    class_a, class_b, total = jnp.int32(none), jnp.int32(none), jnp.int32(0)
    for layer in range(layers):
        for gap in range(owners):
            on = listed(2, layer, gap)
            class_b = jnp.where((on > 0) & (total == 1), layer * owners + gap, class_b)
            class_a = jnp.where((on > 0) & (total == 0), layer * owners + gap, class_a)
            total = total + on
    many = (total > 2).astype(jnp.int32)
    shift_a = jnp.where(class_a < none, lax.rem(class_a, owners), 0)
    shift_b = jnp.where(class_b < none, lax.rem(class_b, owners), 0)
    flip = shift_a > shift_b
    class_a, class_b = jnp.where(flip, class_b, class_a), jnp.where(flip, class_a, class_b)
    shift_a, shift_b = jnp.where(flip, shift_b, shift_a), jnp.where(flip, shift_a, shift_b)
    for number, by in ((class_a, shift_a), (class_b, shift_b)):
        layer = jnp.where(number < none, lax.div(number, owners), 0)
        index = listed(1, layer, lax.rem(me + by, owners))
        fetches.append(fetch(layer, index, len(fetches)))
        fetches[-1].start()
    choice_ref[0] = lax.div(shift_b * (shift_b + 1), 2) + shift_a
    choice_ref[1] = many

    for layer in range(layers):
        for index in range(owners):
            second_ref[layer, index] = listed(1, layer, index)
            slot = listed(3, layer, index)
            plain = jnp.where(slot >= late, slot - late, slot)
            back = lax.rem(me - lax.div(plain, layers) + owners, owners)
            moved = jnp.where(layer * owners + back == class_a, slots, slots + 1)
            moved = jnp.where(many > 0, slots + 2 + plain, moved)
            table_ref[layer, index] = jnp.where(slot >= late, moved, slot)

    targets = [payload_ref.at[k] for k in range(slots)] + [left_ref, right_ref]
    leaves = [
        pltpu.make_async_copy(stage.at[k], target, sem_out.at[k])
        for k, target in enumerate(targets)
    ]
    forward(fetches, leaves)


def plan_and_pack(keep_list, page_slot, cache, owners):
    layers, entries = keep_list.shape
    slots, block = owners * layers, cache.shape[3:]
    page_dev = entries // owners
    vmem = pl.BlockSpec(memory_space=pltpu.VMEM)
    smem = pl.BlockSpec(memory_space=pltpu.SMEM)
    hbm = pl.BlockSpec(memory_space=pltpu.HBM)
    one = jax.ShapeDtypeStruct(block, cache.dtype)
    return pl.pallas_call(
        functools.partial(plan_kernel, owners, cache.shape[1], page_dev),
        in_specs=[vmem, vmem, hbm],
        out_specs=[hbm, hbm, hbm, smem, smem, smem],
        scratch_shapes=[
            pltpu.VMEM((slots + 2, *block), cache.dtype),
            pltpu.VMEM((owners, 128), jnp.int32),
            pltpu.SMEM((owners, 128), jnp.int32),
            pltpu.SemaphoreType.DMA((slots + 2,)),
            pltpu.SemaphoreType.DMA((slots + 2,)),
            pltpu.SemaphoreType.DMA,
        ],
        out_shape=[
            jax.ShapeDtypeStruct((slots, *block), cache.dtype),
            one,
            one,
            jax.ShapeDtypeStruct((layers, page_dev), jnp.int32),
            jax.ShapeDtypeStruct((layers, owners), jnp.int32),
            jax.ShapeDtypeStruct((2,), jnp.int32),
        ],
        compiler_params=pltpu.CompilerParams(vmem_limit_bytes=8 << 20),
    )(keep_list, page_slot, cache)


def place_kernel(
    table_ref, many_ref, base_ref, left_ref, right_ref, extra_ref,
    out_ref, bounds_ref, empty, spare, rows, sem, spare_sem,
):
    pages, slots = out_ref.shape[0], base_ref.shape[0]
    head_width = base_ref.shape[-1] // 2
    empty[...] = jnp.zeros_like(empty)

    @pl.when(many_ref[0] != 0)
    def _():
        copy = pltpu.make_async_copy(extra_ref, spare, spare_sem)
        copy.start()
        copy.wait()

    def put(i, ref):
        pltpu.make_async_copy(ref, out_ref.at[i], sem.at[i]).start()
        keys = ref[:, :head_width].astype(jnp.float32)
        rows[pl.ds(2 * i, 1), :] = jnp.max(keys, axis=0, keepdims=True)
        rows[pl.ds(2 * i + 1, 1), :] = -jnp.min(keys, axis=0, keepdims=True)

    for i in range(pages):
        t = table_ref[i // table_ref.shape[1], i % table_ref.shape[1]]

        @pl.when(t < 0)
        def _():
            pltpu.make_async_copy(empty, out_ref.at[i], sem.at[i]).start()
            rows[pl.ds(2 * i, 2), :] = jnp.zeros((2, head_width), jnp.float32)

        @pl.when((t >= 0) & (t < slots))
        def _():
            put(i, base_ref.at[jnp.clip(t, 0, slots - 1)])

        @pl.when(t == slots)
        def _():
            put(i, left_ref)

        @pl.when(t == slots + 1)
        def _():
            put(i, right_ref)

        @pl.when(t >= slots + 2)
        def _():
            put(i, spare.at[jnp.clip(t - slots - 2, 0, slots - 1)])

    bounds_ref[...] = rows[...].astype(bounds_ref.dtype)
    for i in range(pages):
        pltpu.make_async_copy(empty, out_ref.at[i], sem.at[i]).wait()


def place_pages(table, many, base, left, right, extra, pages):
    block, head_width = base.shape[1:], base.shape[-1] // 2
    vmem = pl.BlockSpec(memory_space=pltpu.VMEM)
    hbm = pl.BlockSpec(memory_space=pltpu.HBM)
    return pl.pallas_call(
        place_kernel,
        grid_spec=pltpu.PrefetchScalarGridSpec(
            num_scalar_prefetch=2,
            grid=(1,),
            in_specs=[vmem, vmem, vmem, hbm],
            out_specs=[hbm, vmem],
            scratch_shapes=[
                pltpu.VMEM(block, base.dtype),
                pltpu.VMEM(base.shape, base.dtype),
                pltpu.VMEM((2 * pages, head_width), jnp.float32),
                pltpu.SemaphoreType.DMA((pages,)),
                pltpu.SemaphoreType.DMA,
            ],
        ),
        out_shape=[
            jax.ShapeDtypeStruct((pages, *block), base.dtype),
            jax.ShapeDtypeStruct((2 * pages, head_width), base.dtype),
        ],
        compiler_params=pltpu.CompilerParams(vmem_limit_bytes=8 << 20),
    )(table, many, base, left, right, extra)


def swap(block, shift, size):
    if shift == 0:
        return block
    return lax.ppermute(block, "seq", [(s, (s + shift) % size) for s in range(size)])


def on_device(kv_cache, keep_list, page_slot):
    layer_count, page_count = keep_list.shape
    seq_count = lax.axis_size("seq")
    page_dev = page_count // seq_count
    slots = seq_count * layer_count

    def exchange(blocks):
        shaped = blocks.reshape(seq_count, layer_count, *blocks.shape[1:])
        moved = lax.all_to_all(shaped, "seq", split_axis=0, concat_axis=0, tiled=True)
        return moved.reshape(blocks.shape)

    payload, one, two, table, second, choice = plan_and_pack(
        keep_list, page_slot, kv_cache, seq_count
    )
    branch, many = choice[0], choice[1]
    base = exchange(payload)

    branches = [
        lambda one, two, one_by=a, two_by=b: (
            swap(one, one_by, seq_count),
            swap(two, two_by, seq_count),
        )
        for b in range(seq_count)
        for a in range(b + 1)
    ]
    left, right = lax.switch(branch, branches, one, two)

    def all_seconds(state):
        rounds, index, _ = lax.optimization_barrier(state)
        return rounds - 1, index, exchange(pack_seconds(index, kv_cache, slots))

    base, payload, many = lax.optimization_barrier((base, payload, many))
    _, _, extra = lax.while_loop(lambda state: state[0] > 0, all_seconds, (many, second, payload))

    pages, half = place_pages(
        table, many.reshape(1), base, left, right, extra, layer_count * page_dev
    )
    halves = lax.all_gather(half, "rep")
    high = jnp.max(halves, axis=0).reshape(layer_count, page_dev, 1, 2, half.shape[-1])
    is_low = lax.broadcasted_iota(jnp.int32, high.shape, 3) == 1
    page_bounds = jnp.where(is_low, 0 - high, high)
    paged_cache = pages.reshape(layer_count, page_dev, *kv_cache.shape[2:])
    return paged_cache, page_bounds


def solution(mesh):
    in_specs = (
        P(None, ("groups", "seq"), "head", "rep", None),
        P("groups", None),
        P("groups", None),
    )
    out_specs = (
        P(None, ("groups", "seq"), "head", "rep", None),
        P(None, ("groups", "seq"), "head", None, None),
    )
    return jax.shard_map(
        on_device, mesh=mesh, in_specs=in_specs, out_specs=out_specs, check_vma=False
    )
```

time: 114 us -> 114 us (level)
  the two profiles are of different devices: /device:TPU:85 before, /device:TPU:65 now
where the time goes in v2:
time: 114 us
  starting transfers between devices  58.2 us (51%)
  waiting for transfers between devices  37.3 us (33%)
  Pallas kernels  7.74 us (7%)
  blocking collectives  5.34 us (5%)
  between operations  2.04 us (2%)
  local copies, waits for them, and re-layouts  2.02 us (2%)
    all_to_all x1, starting transfers between devices, exchange(): lax.all_to_all(shaped, 'seq', split_axis=0, concat_axis=0, tiled=True)  44 us
    ppermute x2, waiting for transfers between devices, swap(): lax.ppermute(block, 'seq', [(s, (s + shift) % size) for s in range(size)])  37.3 us
    ppermute x2, starting transfers between devices, swap(): lax.ppermute(block, 'seq', [(s, (s + shift) % size) for s in range(size)])  14.2 us
    all_gather x1, blocking collectives, on_device(): halves = lax.all_gather(half, 'rep')  5.34 us
    pallas_call x1, Pallas kernels, plan_and_pack(): pl.pallas_call(functools.partial(plan_kernel, owners, cache.shape[1], pag...  4.35 us
    pallas_call x1, Pallas kernels, place_pages(): pl.pallas_call(place_kernel, grid_spec=pltpu.PrefetchScalarGridSpec(num_s...  3.39 us
  transfers between devices with their start and end apart: 3, of which 1 were waited for; matrix products, arithmetic and copies ran while one was open for 1% of the time, Pallas kernels for 0%

profile of v2, /device:TPU:65, one launch (start us, length us, event | category | flops | bytes accessed | tf_op | source)
XLA Modules:
  0.0 113.9 jit_solution(3626169123116648772)
XLA Ops:
  0.6 0.0 copy-start
  0.6 0.7 copy-done
  1.3 0.0 copy-start.1
  1.3 0.7 copy-done.1
  2.0 4.3 %shard_map.50 = (bf16[32,64,256]{2,1,0:T(8,128)(2,1)}, bf16[64,256]{1,0:T(8,128)(2,1)S(1)}, bf16[64,256]{1,0:T(8,128)(2,1)S(1)}, s32[2,16]{1,0:T(2,128)S(1)}, s32[2,16]{1,0:T(2,128)S(1)}, /*index=5*/s32[2]{0:T(128)S(1)}) custom-call(s32[2,256]{1,0:T(2,128)S(1)} %copy-done, s32[2,256]{1,0:T(2,128)S(1)} %copy-done.1, bf16[2,32,1,64,256]{4,3,2,1,0:T(8,128)(2,1)} %cache_ref.1), custom_call_target="tpu_custom_call" | custom-call | tf_op jit(solution)/shard_map/pallas_call | solution.py:165
  6.4 44.0 %all-to-all-start.1 = ((bf16[16,2,64,256]{3,2,1,0:T(8,128)(2,1)}), bf16[16,2,64,256]{3,2,1,0:T(8,128)(2,1)S(1)}, u32[]{:S(2)}, u32[]{:S(2)}) async-start(bf16[16,2,64,256]{3,2,1,0:T(8,128)(2,1)} %bitcast.2), calls=%async_computation.1 | async-start | bytes 2097152 | tf_op jit(solution)/shard_map/all_to_all | solution.py:279
  50.4 0.6 fusion
  51.7 0.0 copy-start.2
  51.7 52.0 %conditional.1 = ((bf16[64,256]{1,0:T(8,128)(2,1)S(1)}, bf16[64,256]{1,0:T(8,128)(2,1)S(1)})) conditional(s32[]{:T(128)} %bitcast.6, (bf16[64,256]{1,0:T(8,128)(2,1)S(1)}, bf16[64,256]{1,0:T(8,128)(2,1)S(1)}) %tuple.570, (bf16[64,256]{1,0:T(8,128)(2,1)S(1)}, bf16[64,256]{1,0:T(8,128)(2,1)S(1)}) %tuple.571, ...), branch_computations={%region_0.0_spmd, %region_1.0_spmd, %region_2.0_spmd, %region_3.0_... | conditional | bytes 393320 | solution.py:296
  52.0 9.3 %collective-permute-start.189 = (bf16[64,256]{1,0:T(8,128)(2,1)S(1)}, bf16[64,256]{1,0:T(8,128)(2,1)S(1)}, u32[]{:S(2)}, u32[]{:S(2)}) collective-permute-start(bf16[64,256]{1,0:T(8,128)(2,1)S(1)} %get-tuple-element.791), channel_id=1, source_target_pairs={{0,176},{16,192},{32,208},{48,224},{64,240},{80,0},{96,16},{112,32... | collective-permute-start | bytes 98312 | tf_op jit(solution)/shard_map/cond/branch_102_fun/ppermute | solution.py:268
  61.2 4.9 %collective-permute-start.190 = (bf16[64,256]{1,0:T(8,128)(2,1)S(1)}, bf16[64,256]{1,0:T(8,128)(2,1)S(1)}, u32[]{:S(2)}, u32[]{:S(2)}) collective-permute-start(bf16[64,256]{1,0:T(8,128)(2,1)S(1)} %get-tuple-element.792), channel_id=1, source_target_pairs={{0,208},{16,224},{32,240},{48,0},{64,16},{80,32},{96,48},{112,64},... | collective-permute-start | bytes 98312 | tf_op jit(solution)/shard_map/cond/branch_102_fun/ppermute | solution.py:268
  66.1 37.3 %collective-permute-done.189 = bf16[64,256]{1,0:T(8,128)(2,1)S(1)} collective-permute-done((bf16[64,256]{1,0:T(8,128)(2,1)S(1)}, bf16[64,256]{1,0:T(8,128)(2,1)S(1)}, u32[]{:S(2)}, u32[]{:S(2)}) %collective-permute-start.189) | collective-permute-done | bytes 32800 | tf_op jit(solution)/shard_map/cond/branch_102_fun/ppermute | solution.py:268
  103.4 0.0 collective-permute-done.190
  103.7 0.0 all-to-all-done.1
  104.4 0.0 copy-done.2
  104.4 3.4 %shard_map.51 = (bf16[32,64,256]{2,1,0:T(8,128)(2,1)}, bf16[64,128]{1,0:T(8,128)(2,1)S(1)}) custom-call(s32[2,16]{1,0:T(2,128)S(1)} %get-tuple-element.881.table_ref, s32[1]{0:T(128)} %bitcast.5.many_ref, bf16[32,64,256]{2,1,0:T(8,128)(2,1)S(1)} %bitcast.16, bf16[64,256]{1,0:T(8,128)(2,1)S(1)} %get-tuple-element.888.left_ref, ...), custom_call_target="tpu_custom_call" | custom-call | tf_op jit(solution)/shard_map/pallas_call | solution.py:242
  107.8 5.3 %all-gather = bf16[128,128]{1,0:T(8,128)(2,1)S(1)} all-gather(bf16[64,128]{1,0:T(8,128)(2,1)S(1)} %get-tuple-element.894), channel_id=2, replica_groups=mesh['groups'=2,'seq'=16,'head'=8,'rep'=2] {'rep'}, dimensions={0}, use_global_device_ids=true | all-gather | bytes 49152 | tf_op jit(solution)/shard_map/all_gather | solution.py:308
  113.2 0.7 broadcast_select_fusion
  (5 shorter events, 0.0 us)
Async XLA Ops:
  0.6 0.7 copy-start
  1.3 0.7 copy-start.1
  6.4 97.4 %all-to-all-start.1 = ((bf16[16,2,64,256]{3,2,1,0:T(8,128)(2,1)}), bf16[16,2,64,256]{3,2,1,0:T(8,128)(2,1)S(1)}, u32[]{:S(2)}, u32[]{:S(2)}) async-start(bf16[16,2,64,256]{3,2,1,0:T(8,128)(2,1)} %bitcast.2), calls=%async_computation.1 | async-start | bytes 2097152 | tf_op jit(solution)/shard_map/all_to_all | solution.py:279
  51.7 52.7 %copy-start.2 = (bf16[2,32,1,64,256]{4,3,2,1,0:T(8,128)(2,1)S(1)}, bf16[2,32,1,64,256]{4,3,2,1,0:T(8,128)(2,1)}, u32[]{:S(2)}) copy-start(bf16[2,32,1,64,256]{4,3,2,1,0:T(8,128)(2,1)} %cache_ref.1) | copy-start | bytes 6291460
  52.0 51.5 %collective-permute-start.189 = (bf16[64,256]{1,0:T(8,128)(2,1)S(1)}, bf16[64,256]{1,0:T(8,128)(2,1)S(1)}, u32[]{:S(2)}, u32[]{:S(2)}) collective-permute-start(bf16[64,256]{1,0:T(8,128)(2,1)S(1)} %get-tuple-element.791), channel_id=1, source_target_pairs={{0,176},{16,192},{32,208},{48,224},{64,240},{80,0},{96,16},{112,32... | collective-permute-start | bytes 98312 | tf_op jit(solution)/shard_map/cond/branch_102_fun/ppermute | solution.py:268
  61.2 42.2 %collective-permute-start.190 = (bf16[64,256]{1,0:T(8,128)(2,1)S(1)}, bf16[64,256]{1,0:T(8,128)(2,1)S(1)}, u32[]{:S(2)}, u32[]{:S(2)}) collective-permute-start(bf16[64,256]{1,0:T(8,128)(2,1)S(1)} %get-tuple-element.792), channel_id=1, source_target_pairs={{0,208},{16,224},{32,240},{48,0},{64,16},{80,32},{96,48},{112,64},... | collective-permute-start | bytes 98312 | tf_op jit(solution)/shard_map/cond/branch_102_fun/ppermute | solution.py:268

commit v3 on v2

--- a/solution.py
+++ b/solution.py
@@ -55,10 +55,16 @@
 
 def plan_kernel(
     owners, blk_dev, page_dev,
-    keep_ref, slot_ref, cache_ref,
-    payload_ref, left_ref, right_ref, table_ref, second_ref, choice_ref,
-    stage, lists, held_lists, sem_in, sem_out, sem_list,
+    keep_hbm, slot_hbm, cache_ref,
+    payload_ref, left_ref, right_ref, table_ref, second_ref, branch_ref, many_ref,
+    keep_ref, slot_ref, stage, lists, held_lists, sem_in, sem_out, sem_list,
 ):
+    inputs = [
+        pltpu.make_async_copy(keep_hbm, keep_ref, sem_in.at[0]),
+        pltpu.make_async_copy(slot_hbm, slot_ref, sem_in.at[1]),
+    ]
+    for copy in inputs:
+        copy.start()
     layers, entries = keep_ref.shape
     slots, none = owners * layers, 2 * owners * layers
     late = 8 * slots
@@ -73,6 +79,8 @@
     def most(values):
         return jnp.max(values.astype(jnp.float32), axis=1, keepdims=True).astype(jnp.int32)
 
+    for copy in inputs:
+        copy.wait()
     tables = jnp.zeros(lists.shape, jnp.int32)
     for layer in range(layers):
         keep, slot = keep_ref[pl.ds(layer, 1), :], slot_ref[pl.ds(layer, 1), :]
@@ -133,8 +141,8 @@
         index = listed(1, layer, lax.rem(me + by, owners))
         fetches.append(fetch(layer, index, len(fetches)))
         fetches[-1].start()
-    choice_ref[0] = lax.div(shift_b * (shift_b + 1), 2) + shift_a
-    choice_ref[1] = many
+    branch_ref[0] = lax.div(shift_b * (shift_b + 1), 2) + shift_a
+    many_ref[0] = many
 
     for layer in range(layers):
         for index in range(owners):
@@ -143,8 +151,9 @@
             plain = jnp.where(slot >= late, slot - late, slot)
             back = lax.rem(me - lax.div(plain, layers) + owners, owners)
             moved = jnp.where(layer * owners + back == class_a, slots, slots + 1)
-            moved = jnp.where(many > 0, slots + 2 + plain, moved)
-            table_ref[layer, index] = jnp.where(slot >= late, moved, slot)
+            moved = jnp.where(many > 0, slots + 3 + plain, moved)
+            moved = jnp.where(slot >= late, moved, slot)
+            table_ref[layer, index] = jnp.where(slot < 0, slots + 2, moved)
 
     targets = [payload_ref.at[k] for k in range(slots)] + [left_ref, right_ref]
     leaves = [
@@ -158,15 +167,16 @@
     layers, entries = keep_list.shape
     slots, block = owners * layers, cache.shape[3:]
     page_dev = entries // owners
-    vmem = pl.BlockSpec(memory_space=pltpu.VMEM)
     smem = pl.BlockSpec(memory_space=pltpu.SMEM)
     hbm = pl.BlockSpec(memory_space=pltpu.HBM)
     one = jax.ShapeDtypeStruct(block, cache.dtype)
     return pl.pallas_call(
         functools.partial(plan_kernel, owners, cache.shape[1], page_dev),
-        in_specs=[vmem, vmem, hbm],
-        out_specs=[hbm, hbm, hbm, smem, smem, smem],
+        in_specs=[hbm, hbm, hbm],
+        out_specs=[hbm, hbm, hbm, smem, smem, smem, smem],
         scratch_shapes=[
+            pltpu.VMEM(keep_list.shape, jnp.int32),
+            pltpu.VMEM(page_slot.shape, jnp.int32),
             pltpu.VMEM((slots + 2, *block), cache.dtype),
             pltpu.VMEM((owners, 128), jnp.int32),
             pltpu.SMEM((owners, 128), jnp.int32),
@@ -180,59 +190,68 @@
             one,
             jax.ShapeDtypeStruct((layers, page_dev), jnp.int32),
             jax.ShapeDtypeStruct((layers, owners), jnp.int32),
-            jax.ShapeDtypeStruct((2,), jnp.int32),
+            jax.ShapeDtypeStruct((1,), jnp.int32),
+            jax.ShapeDtypeStruct((1,), jnp.int32),
         ],
-        compiler_params=pltpu.CompilerParams(vmem_limit_bytes=8 << 20),
+        compiler_params=pltpu.CompilerParams(vmem_limit_bytes=60 << 20),
     )(keep_list, page_slot, cache)
 
 
 def place_kernel(
     table_ref, many_ref, base_ref, left_ref, right_ref, extra_ref,
-    out_ref, bounds_ref, empty, spare, rows, sem, spare_sem,
+    out_ref, bounds_ref, spare, high, low, rows, sem, spare_sem,
 ):
-    pages, slots = out_ref.shape[0], base_ref.shape[0]
-    head_width = base_ref.shape[-1] // 2
-    empty[...] = jnp.zeros_like(empty)
+    layers, page_dev = table_ref.shape
+    slots, head_width = base_ref.shape[0], base_ref.shape[-1] // 2
+    pages = layers * page_dev
+    spare[0] = left_ref[...]
+    spare[1] = right_ref[...]
+    spare[2] = jnp.zeros_like(left_ref)
+
+    def entry(i):
+        return table_ref[i // page_dev, i % page_dev]
+
+    for i in range(pages):
+        t = entry(i)
+
+        @pl.when(t < slots)
+        def _():
+            block = base_ref.at[jnp.minimum(t, slots - 1)]
+            pltpu.make_async_copy(block, out_ref.at[i], sem).start()
+
+    def extremes(k, ref):
+        keys = ref[:, :head_width]
+        high[pl.ds(k, 1), :] = jnp.max(keys, axis=0, keepdims=True).astype(jnp.float32)
+        low[pl.ds(k, 1), :] = -jnp.min(keys, axis=0, keepdims=True).astype(jnp.float32)
+
+    for k in range(slots):
+        extremes(k, base_ref.at[k])
+    for k in range(3):
+        extremes(slots + k, spare.at[k])
 
     @pl.when(many_ref[0] != 0)
     def _():
-        copy = pltpu.make_async_copy(extra_ref, spare, spare_sem)
+        copy = pltpu.make_async_copy(extra_ref, spare.at[pl.ds(3, slots)], spare_sem)
         copy.start()
         copy.wait()
 
-    def put(i, ref):
-        pltpu.make_async_copy(ref, out_ref.at[i], sem.at[i]).start()
-        keys = ref[:, :head_width].astype(jnp.float32)
-        rows[pl.ds(2 * i, 1), :] = jnp.max(keys, axis=0, keepdims=True)
-        rows[pl.ds(2 * i + 1, 1), :] = -jnp.min(keys, axis=0, keepdims=True)
+        @pl.loop(0, slots)
+        def _(k):
+            extremes(slots + 3 + k, spare.at[3 + k])
 
     for i in range(pages):
-        t = table_ref[i // table_ref.shape[1], i % table_ref.shape[1]]
-
-        @pl.when(t < 0)
+        t = entry(i)
+
+        @pl.when(t >= slots)
         def _():
-            pltpu.make_async_copy(empty, out_ref.at[i], sem.at[i]).start()
-            rows[pl.ds(2 * i, 2), :] = jnp.zeros((2, head_width), jnp.float32)
-
-        @pl.when((t >= 0) & (t < slots))
-        def _():
-            put(i, base_ref.at[jnp.clip(t, 0, slots - 1)])
-
-        @pl.when(t == slots)
-        def _():
-            put(i, left_ref)
-
-        @pl.when(t == slots + 1)
-        def _():
-            put(i, right_ref)
-
-        @pl.when(t >= slots + 2)
-        def _():
-            put(i, spare.at[jnp.clip(t - slots - 2, 0, slots - 1)])
+            block = spare.at[jnp.maximum(t - slots, 0)]
+            pltpu.make_async_copy(block, out_ref.at[i], sem).start()
+
+        rows[pl.ds(2 * i, 1), :] = high[pl.ds(t, 1), :]
+        rows[pl.ds(2 * i + 1, 1), :] = low[pl.ds(t, 1), :]
 
     bounds_ref[...] = rows[...].astype(bounds_ref.dtype)
-    for i in range(pages):
-        pltpu.make_async_copy(empty, out_ref.at[i], sem.at[i]).wait()
+    pltpu.make_async_copy(out_ref, out_ref, sem).wait()
 
 
 def place_pages(table, many, base, left, right, extra, pages):
@@ -247,10 +266,11 @@
             in_specs=[vmem, vmem, vmem, hbm],
             out_specs=[hbm, vmem],
             scratch_shapes=[
-                pltpu.VMEM(block, base.dtype),
-                pltpu.VMEM(base.shape, base.dtype),
+                pltpu.VMEM((3 + base.shape[0], *block), base.dtype),
+                pltpu.VMEM((3 + 2 * base.shape[0], head_width), jnp.float32),
+                pltpu.VMEM((3 + 2 * base.shape[0], head_width), jnp.float32),
                 pltpu.VMEM((2 * pages, head_width), jnp.float32),
-                pltpu.SemaphoreType.DMA((pages,)),
+                pltpu.SemaphoreType.DMA,
                 pltpu.SemaphoreType.DMA,
             ],
         ),
@@ -279,10 +299,10 @@
         moved = lax.all_to_all(shaped, "seq", split_axis=0, concat_axis=0, tiled=True)
         return moved.reshape(blocks.shape)
 
-    payload, one, two, table, second, choice = plan_and_pack(
+    payload, one, two, table, second, branch, many = plan_and_pack(
         keep_list, page_slot, kv_cache, seq_count
     )
-    branch, many = choice[0], choice[1]
+    branch, many = branch.reshape(()), many.reshape(())
     base = exchange(payload)
 
     branches = [

time: 114 us -> 113 us (level)
  the two profiles are of different devices: /device:TPU:65 before, /device:TPU:81 now
where the time goes in v3:
time: 113 us; the launch traced here: 112 us
  starting transfers between devices  57.5 us (51%)
  waiting for transfers between devices  38.3 us (34%)
  Pallas kernels  7.13 us (6%)
  blocking collectives  5.78 us (5%)
  between operations  2.04 us (2%)
    all_to_all x1, starting transfers between devices, exchange(): lax.all_to_all(shaped, 'seq', split_axis=0, concat_axis=0, tiled=True)  43.3 us
    ppermute x2, waiting for transfers between devices, swap(): lax.ppermute(block, 'seq', [(s, (s + shift) % size) for s in range(size)])  38.3 us
    ppermute x2, starting transfers between devices, swap(): lax.ppermute(block, 'seq', [(s, (s + shift) % size) for s in range(size)])  14.2 us
    all_gather x1, blocking collectives, on_device(): halves = lax.all_gather(half, 'rep')  5.78 us
    pallas_call x1, Pallas kernels, plan_and_pack(): pl.pallas_call(functools.partial(plan_kernel, owners, cache.shape[1], pag...  4.93 us
  transfers between devices with their start and end apart: 3, of which 2 were waited for; matrix products, arithmetic and copies ran while one was open for 0% of the time, Pallas kernels for 0%

profile of v3, /device:TPU:81, one launch (start us, length us, event | category | flops | bytes accessed | tf_op | source)
XLA Modules:
  0.0 112.4 jit_solution(6990358602067532198)
XLA Ops:
  0.6 4.9 %shard_map.50 = (bf16[32,64,256]{2,1,0:T(8,128)(2,1)}, bf16[64,256]{1,0:T(8,128)(2,1)S(1)}, bf16[64,256]{1,0:T(8,128)(2,1)S(1)}, s32[2,16]{1,0:T(2,128)}, s32[2,...) custom-call(s32[2,256]{1,0:T(2,128)} %keep_hbm.1, s32[2,256]{1,0:T(2,128)} %slot_hbm.1, bf16[2,32,1,64,256]{4,3,2,1,0:T(8,128)(2,1)} %cache_ref.1), custom_call_target="tpu_custom_call" | custom-call | tf_op jit(solution)/shard_map/pallas_call | solution.py:173
  5.6 43.3 %all-to-all-start.1 = ((bf16[16,2,64,256]{3,2,1,0:T(8,128)(2,1)}), bf16[16,2,64,256]{3,2,1,0:T(8,128)(2,1)S(1)}, u32[]{:S(2)}, u32[]{:S(2)}) async-start(bf16[16,2,64,256]{3,2,1,0:T(8,128)(2,1)} %bitcast.2), calls=%async_computation.1 | async-start | bytes 2097152 | tf_op jit(solution)/shard_map/all_to_all | solution.py:299
  49.5 0.0 copy-start.1
  49.5 52.8 %conditional.1 = ((bf16[64,256]{1,0:T(8,128)(2,1)S(1)}, bf16[64,256]{1,0:T(8,128)(2,1)S(1)})) conditional(s32[]{:T(128)} %bitcast.6, (bf16[64,256]{1,0:T(8,128)(2,1)S(1)}, bf16[64,256]{1,0:T(8,128)(2,1)S(1)}) %tuple.570, (bf16[64,256]{1,0:T(8,128)(2,1)S(1)}, bf16[64,256]{1,0:T(8,128)(2,1)S(1)}) %tuple.571, ...), branch_computations={%region_0.0_spmd, %region_1.0_spmd, %region_2.0_spmd, %region_3.0_... | conditional | bytes 393320 | solution.py:316
  49.8 10.2 %collective-permute-start.162 = (bf16[64,256]{1,0:T(8,128)(2,1)S(1)}, bf16[64,256]{1,0:T(8,128)(2,1)S(1)}, u32[]{:S(2)}, u32[]{:S(2)}) collective-permute-start(bf16[64,256]{1,0:T(8,128)(2,1)S(1)} %get-tuple-element.763), channel_id=1, source_target_pairs={{0,160},{16,176},{32,192},{48,208},{64,224},{80,240},{96,0},{112,1... | collective-permute-start | bytes 98312 | tf_op jit(solution)/shard_map/cond/branch_88_fun/ppermute | solution.py:288
  60.0 4.0 %collective-permute-start.163 = (bf16[64,256]{1,0:T(8,128)(2,1)S(1)}, bf16[64,256]{1,0:T(8,128)(2,1)S(1)}, u32[]{:S(2)}, u32[]{:S(2)}) collective-permute-start(bf16[64,256]{1,0:T(8,128)(2,1)S(1)} %get-tuple-element.764), channel_id=1, source_target_pairs={{0,192},{16,208},{32,224},{48,240},{64,0},{80,16},{96,32},{112,48}... | collective-permute-start | bytes 98312 | tf_op jit(solution)/shard_map/cond/branch_88_fun/ppermute | solution.py:288
  64.0 36.9 %collective-permute-done.162 = bf16[64,256]{1,0:T(8,128)(2,1)S(1)} collective-permute-done((bf16[64,256]{1,0:T(8,128)(2,1)S(1)}, bf16[64,256]{1,0:T(8,128)(2,1)S(1)}, u32[]{:S(2)}, u32[]{:S(2)}) %collective-permute-start.162) | collective-permute-done | bytes 32800 | tf_op jit(solution)/shard_map/cond/branch_88_fun/ppermute | solution.py:288
  100.9 1.5 %collective-permute-done.163 = bf16[64,256]{1,0:T(8,128)(2,1)S(1)} collective-permute-done((bf16[64,256]{1,0:T(8,128)(2,1)S(1)}, bf16[64,256]{1,0:T(8,128)(2,1)S(1)}, u32[]{:S(2)}, u32[]{:S(2)}) %collective-permute-start.163) | collective-permute-done | bytes 32800 | tf_op jit(solution)/shard_map/cond/branch_88_fun/ppermute | solution.py:288
  102.3 0.0 all-to-all-done.1
  103.0 0.0 copy-done.1
  103.0 0.0 copy-start
  103.1 0.7 copy-done
  103.7 2.2 %shard_map.51 = (bf16[32,64,256]{2,1,0:T(8,128)(2,1)}, bf16[64,128]{1,0:T(8,128)(2,1)S(1)}) custom-call(s32[2,16]{1,0:T(2,128)S(1)} %copy-done, s32[1]{0:T(128)} %bitcast.5.many_ref, bf16[32,64,256]{2,1,0:T(8,128)(2,1)S(1)} %bitcast.16, bf16[64,256]{1,0:T(8,128)(2,1)S(1)} %get-tuple-element.890.left_ref, bf16[64,256]{1,0:T(8,128)(2,1)S(1)} %get-tuple-element.891.right_ref, ...), custom_call_target="tpu_custom_call" | custom-call | tf_op jit(solution)/shard_map/pallas_call | solution.py:261
  105.9 5.8 %all-gather = bf16[128,128]{1,0:T(8,128)(2,1)S(1)} all-gather(bf16[64,128]{1,0:T(8,128)(2,1)S(1)} %get-tuple-element.896), channel_id=2, replica_groups=mesh['groups'=2,'seq'=16,'head'=8,'rep'=2] {'rep'}, dimensions={0}, use_global_device_ids=true | all-gather | bytes 49152 | tf_op jit(solution)/shard_map/all_gather | solution.py:328
  111.7 0.7 broadcast_select_fusion
  (5 shorter events, 0.0 us)
Async XLA Ops:
  5.6 96.8 %all-to-all-start.1 = ((bf16[16,2,64,256]{3,2,1,0:T(8,128)(2,1)}), bf16[16,2,64,256]{3,2,1,0:T(8,128)(2,1)S(1)}, u32[]{:S(2)}, u32[]{:S(2)}) async-start(bf16[16,2,64,256]{3,2,1,0:T(8,128)(2,1)} %bitcast.2), calls=%async_computation.1 | async-start | bytes 2097152 | tf_op jit(solution)/shard_map/all_to_all | solution.py:299
  49.5 53.5 %copy-start.1 = (bf16[2,32,1,64,256]{4,3,2,1,0:T(8,128)(2,1)S(1)}, bf16[2,32,1,64,256]{4,3,2,1,0:T(8,128)(2,1)}, u32[]{:S(2)}) copy-start(bf16[2,32,1,64,256]{4,3,2,1,0:T(8,128)(2,1)} %cache_ref.1) | copy-start | bytes 6291460
  49.8 51.1 %collective-permute-start.162 = (bf16[64,256]{1,0:T(8,128)(2,1)S(1)}, bf16[64,256]{1,0:T(8,128)(2,1)S(1)}, u32[]{:S(2)}, u32[]{:S(2)}) collective-permute-start(bf16[64,256]{1,0:T(8,128)(2,1)S(1)} %get-tuple-element.763), channel_id=1, source_target_pairs={{0,160},{16,176},{32,192},{48,208},{64,224},{80,240},{96,0},{112,1... | collective-permute-start | bytes 98312 | tf_op jit(solution)/shard_map/cond/branch_88_fun/ppermute | solution.py:288
  60.0 42.4 %collective-permute-start.163 = (bf16[64,256]{1,0:T(8,128)(2,1)S(1)}, bf16[64,256]{1,0:T(8,128)(2,1)S(1)}, u32[]{:S(2)}, u32[]{:S(2)}) collective-permute-start(bf16[64,256]{1,0:T(8,128)(2,1)S(1)} %get-tuple-element.764), channel_id=1, source_target_pairs={{0,192},{16,208},{32,224},{48,240},{64,0},{80,16},{96,32},{112,48}... | collective-permute-start | bytes 98312 | tf_op jit(solution)/shard_map/cond/branch_88_fun/ppermute | solution.py:288
  103.0 0.7 copy-start

commit v4 on v3

--- a/solution.py
+++ b/solution.py
@@ -17,11 +17,13 @@
 
 
 def pack_kernel(index_ref, cache_ref, out_ref, stage, sem_in, sem_out):
-    layers, owners = index_ref.shape
+    layers = index_ref.shape[0]
+    owners = out_ref.shape[0] // layers
+    offset = index_ref.shape[1] - owners
     keys = [(layer, owner) for owner in range(owners) for layer in range(layers)]
     fetches = [
         pltpu.make_async_copy(
-            cache_ref.at[layer, index_ref[layer, owner], 0], stage.at[k], sem_in.at[k]
+            cache_ref.at[layer, index_ref[layer, offset + owner], 0], stage.at[k], sem_in.at[k]
         )
         for k, (layer, owner) in enumerate(keys)
     ]
@@ -56,14 +58,27 @@
 def plan_kernel(
     owners, blk_dev, page_dev,
     keep_hbm, slot_hbm, cache_ref,
-    payload_ref, left_ref, right_ref, table_ref, second_ref, branch_ref, many_ref,
-    keep_ref, slot_ref, stage, lists, held_lists, sem_in, sem_out, sem_list,
+    payload_ref, left_ref, right_ref, table_ref, branch_ref, many_ref,
+    keep_ref, slot_ref, shard, lists, held_lists, sem_in, sem_shard, sem_out, sem_list,
 ):
     inputs = [
         pltpu.make_async_copy(keep_hbm, keep_ref, sem_in.at[0]),
         pltpu.make_async_copy(slot_hbm, slot_ref, sem_in.at[1]),
     ]
     for copy in inputs:
+        copy.start()
+    parts = sem_shard.shape[1]
+    size = blk_dev // parts
+    shards = []
+    for layer in range(cache_ref.shape[0]):
+        for part in range(parts):
+            which = (layer, pl.ds(part * size, size))
+            shards.append(
+                pltpu.make_async_copy(
+                    cache_ref.at[which], shard.at[which], sem_shard.at[layer, part]
+                )
+            )
+    for copy in shards:
         copy.start()
     layers, entries = keep_ref.shape
     slots, none = owners * layers, 2 * owners * layers
@@ -114,14 +129,13 @@
     def listed(kind, layer, index):
         return held_lists[index, kind * layers + layer]
 
-    def fetch(layer, index, k):
-        return pltpu.make_async_copy(cache_ref.at[layer, index, 0], stage.at[k], sem_in.at[k])
-
-    fetches = []
+    for copy in shards:
+        copy.wait()
     for owner in range(owners):
         for layer in range(layers):
-            fetches.append(fetch(layer, listed(0, layer, owner), len(fetches)))
-            fetches[-1].start()
+            block = shard.at[layer, listed(0, layer, owner), 0]
+            target = payload_ref.at[owner * layers + layer]
+            pltpu.make_async_copy(block, target, sem_out.at[0]).start()
 
     class_a, class_b, total = jnp.int32(none), jnp.int32(none), jnp.int32(0)
     for layer in range(layers):
@@ -136,17 +150,19 @@
     flip = shift_a > shift_b
     class_a, class_b = jnp.where(flip, class_b, class_a), jnp.where(flip, class_a, class_b)
     shift_a, shift_b = jnp.where(flip, shift_b, shift_a), jnp.where(flip, shift_a, shift_b)
-    for number, by in ((class_a, shift_a), (class_b, shift_b)):
+    extras = []
+    for number, by, target in ((class_a, shift_a, left_ref), (class_b, shift_b, right_ref)):
         layer = jnp.where(number < none, lax.div(number, owners), 0)
         index = listed(1, layer, lax.rem(me + by, owners))
-        fetches.append(fetch(layer, index, len(fetches)))
-        fetches[-1].start()
+        sem = sem_out.at[1 + len(extras)]
+        extras.append(pltpu.make_async_copy(shard.at[layer, index, 0], target, sem))
+        extras[-1].start()
     branch_ref[0] = lax.div(shift_b * (shift_b + 1), 2) + shift_a
     many_ref[0] = many
 
     for layer in range(layers):
         for index in range(owners):
-            second_ref[layer, index] = listed(1, layer, index)
+            table_ref[layer, page_dev + index] = listed(1, layer, index)
             slot = listed(3, layer, index)
             plain = jnp.where(slot >= late, slot - late, slot)
             back = lax.rem(me - lax.div(plain, layers) + owners, owners)
@@ -155,12 +171,9 @@
             moved = jnp.where(slot >= late, moved, slot)
             table_ref[layer, index] = jnp.where(slot < 0, slots + 2, moved)
 
-    targets = [payload_ref.at[k] for k in range(slots)] + [left_ref, right_ref]
-    leaves = [
-        pltpu.make_async_copy(stage.at[k], target, sem_out.at[k])
-        for k, target in enumerate(targets)
-    ]
-    forward(fetches, leaves)
+    pltpu.make_async_copy(payload_ref, payload_ref, sem_out.at[0]).wait()
+    for copy in extras:
+        copy.wait()
 
 
 def plan_and_pack(keep_list, page_slot, cache, owners):
@@ -173,23 +186,23 @@
     return pl.pallas_call(
         functools.partial(plan_kernel, owners, cache.shape[1], page_dev),
         in_specs=[hbm, hbm, hbm],
-        out_specs=[hbm, hbm, hbm, smem, smem, smem, smem],
+        out_specs=[hbm, hbm, hbm, smem, smem, smem],
         scratch_shapes=[
             pltpu.VMEM(keep_list.shape, jnp.int32),
             pltpu.VMEM(page_slot.shape, jnp.int32),
-            pltpu.VMEM((slots + 2, *block), cache.dtype),
+            pltpu.VMEM(cache.shape, cache.dtype),
             pltpu.VMEM((owners, 128), jnp.int32),
             pltpu.SMEM((owners, 128), jnp.int32),
-            pltpu.SemaphoreType.DMA((slots + 2,)),
-            pltpu.SemaphoreType.DMA((slots + 2,)),
+            pltpu.SemaphoreType.DMA((2,)),
+            pltpu.SemaphoreType.DMA((layers, 4)),
+            pltpu.SemaphoreType.DMA((3,)),
             pltpu.SemaphoreType.DMA,
         ],
         out_shape=[
             jax.ShapeDtypeStruct((slots, *block), cache.dtype),
             one,
             one,
-            jax.ShapeDtypeStruct((layers, page_dev), jnp.int32),
-            jax.ShapeDtypeStruct((layers, owners), jnp.int32),
+            jax.ShapeDtypeStruct((layers, page_dev + owners), jnp.int32),
             jax.ShapeDtypeStruct((1,), jnp.int32),
             jax.ShapeDtypeStruct((1,), jnp.int32),
         ],
@@ -201,9 +214,9 @@
     table_ref, many_ref, base_ref, left_ref, right_ref, extra_ref,
     out_ref, bounds_ref, spare, high, low, rows, sem, spare_sem,
 ):
-    layers, page_dev = table_ref.shape
     slots, head_width = base_ref.shape[0], base_ref.shape[-1] // 2
-    pages = layers * page_dev
+    pages = out_ref.shape[0]
+    page_dev = pages // table_ref.shape[0]
     spare[0] = left_ref[...]
     spare[1] = right_ref[...]
     spare[2] = jnp.zeros_like(left_ref)
@@ -299,7 +312,7 @@
         moved = lax.all_to_all(shaped, "seq", split_axis=0, concat_axis=0, tiled=True)
         return moved.reshape(blocks.shape)
 
-    payload, one, two, table, second, branch, many = plan_and_pack(
+    payload, one, two, table, branch, many = plan_and_pack(
         keep_list, page_slot, kv_cache, seq_count
     )
     branch, many = branch.reshape(()), many.reshape(())
@@ -320,7 +333,7 @@
         return rounds - 1, index, exchange(pack_seconds(index, kv_cache, slots))
 
     base, payload, many = lax.optimization_barrier((base, payload, many))
-    _, _, extra = lax.while_loop(lambda state: state[0] > 0, all_seconds, (many, second, payload))
+    _, table, extra = lax.while_loop(lambda state: state[0] > 0, all_seconds, (many, table, payload))
 
     pages, half = place_pages(
         table, many.reshape(1), base, left, right, extra, layer_count * page_dev

time: 113 us -> 109 us (0.965)
  the two profiles are of different devices: /device:TPU:81 before, /device:TPU:65 now
where the time goes in v4:
time: 109 us
  starting transfers between devices  57.5 us (53%)
  waiting for transfers between devices  36.4 us (33%)
  blocking collectives  6.49 us (6%)
  Pallas kernels  6.01 us (6%)
  between operations  1.91 us (2%)
    all_to_all x1, starting transfers between devices, exchange(): lax.all_to_all(shaped, 'seq', split_axis=0, concat_axis=0, tiled=True)  44.2 us
    ppermute x2, waiting for transfers between devices, swap(): lax.ppermute(block, 'seq', [(s, (s + shift) % size) for s in range(size)])  36.4 us
    ppermute x2, starting transfers between devices, swap(): lax.ppermute(block, 'seq', [(s, (s + shift) % size) for s in range(size)])  13.3 us
    all_gather x1, blocking collectives, on_device(): halves = lax.all_gather(half, 'rep')  6.49 us
    pallas_call x1, Pallas kernels, plan_and_pack(): pl.pallas_call(functools.partial(plan_kernel, owners, cache.shape[1], pag...  3.92 us
  transfers between devices with their start and end apart: 3, of which 2 were waited for; matrix products, arithmetic and copies ran while one was open for 0% of the time, Pallas kernels for 0%

profile of v4, /device:TPU:65, one launch (start us, length us, event | category | flops | bytes accessed | tf_op | source)
XLA Modules:
  0.0 109.1 jit_solution(3980444564946693722)
XLA Ops:
  0.6 3.9 %shard_map.50 = (bf16[32,64,256]{2,1,0:T(8,128)(2,1)}, bf16[64,256]{1,0:T(8,128)(2,1)S(1)}, bf16[64,256]{1,0:T(8,128)(2,1)S(1)}, s32[2,32]{1,0:T(2,128)S(1)}, s32[1]{0:T(128)}, /*index=5*/s32[1]{0:T(128)}) custom-call(s32[2,256]{1,0:T(2,128)} %keep_hbm.1, s32[2,256]{1,0:T(2,128)} %slot_hbm.1, bf16[2,32,1,64,256]{4,3,2,1,0:T(8,128)(2,1)} %cache_ref.1), custom_call_target="tpu_custom_call" | custom-call | tf_op jit(solution)/shard_map/pallas_call | solution.py:186
  4.6 44.2 %all-to-all-start.1 = ((bf16[16,2,64,256]{3,2,1,0:T(8,128)(2,1)}), bf16[16,2,64,256]{3,2,1,0:T(8,128)(2,1)S(1)}, u32[]{:S(2)}, u32[]{:S(2)}) async-start(bf16[16,2,64,256]{3,2,1,0:T(8,128)(2,1)} %bitcast.2), calls=%async_computation.1 | async-start | bytes 2097152 | tf_op jit(solution)/shard_map/all_to_all | solution.py:312
  49.4 0.0 copy-start
  49.5 49.8 %conditional.1 = ((bf16[64,256]{1,0:T(8,128)(2,1)S(1)}, bf16[64,256]{1,0:T(8,128)(2,1)S(1)})) conditional(s32[]{:T(128)} %bitcast.6, (bf16[64,256]{1,0:T(8,128)(2,1)S(1)}, bf16[64,256]{1,0:T(8,128)(2,1)S(1)}) %tuple.571, (bf16[64,256]{1,0:T(8,128)(2,1)S(1)}, bf16[64,256]{1,0:T(8,128)(2,1)S(1)}) %tuple.572, ...), branch_computations={%region_2.0_spmd, %region_3.0_spmd, %region_4.0_spmd, %region_5.0_... | conditional | bytes 393320 | solution.py:329
  49.5 7.1 %collective-permute-start.87 = (bf16[64,256]{1,0:T(8,128)(2,1)S(1)}, bf16[64,256]{1,0:T(8,128)(2,1)S(1)}, u32[]{:S(2)}, u32[]{:S(2)}) collective-permute-start(bf16[64,256]{1,0:T(8,128)(2,1)S(1)} %get-tuple-element.691), channel_id=1, source_target_pairs={{0,64},{16,80},{32,96},{48,112},{64,128},{80,144},{96,160},{112,17... | collective-permute-start | bytes 98312 | tf_op jit(solution)/shard_map/cond/branch_49_fun/ppermute | solution.py:301
  56.7 6.1 %collective-permute-start.88 = (bf16[64,256]{1,0:T(8,128)(2,1)S(1)}, bf16[64,256]{1,0:T(8,128)(2,1)S(1)}, u32[]{:S(2)}, u32[]{:S(2)}) collective-permute-start(bf16[64,256]{1,0:T(8,128)(2,1)S(1)} %get-tuple-element.692), channel_id=1, source_target_pairs={{0,144},{16,160},{32,176},{48,192},{64,208},{80,224},{96,240},{112... | collective-permute-start | bytes 98312 | tf_op jit(solution)/shard_map/cond/branch_49_fun/ppermute | solution.py:301
  62.8 27.8 %collective-permute-done.87 = bf16[64,256]{1,0:T(8,128)(2,1)S(1)} collective-permute-done((bf16[64,256]{1,0:T(8,128)(2,1)S(1)}, bf16[64,256]{1,0:T(8,128)(2,1)S(1)}, u32[]{:S(2)}, u32[]{:S(2)}) %collective-permute-start.87) | collective-permute-done | bytes 32800 | tf_op jit(solution)/shard_map/cond/branch_49_fun/ppermute | solution.py:301
  90.6 8.6 %collective-permute-done.88 = bf16[64,256]{1,0:T(8,128)(2,1)S(1)} collective-permute-done((bf16[64,256]{1,0:T(8,128)(2,1)S(1)}, bf16[64,256]{1,0:T(8,128)(2,1)S(1)}, u32[]{:S(2)}, u32[]{:S(2)}) %collective-permute-start.88) | collective-permute-done | bytes 32800 | tf_op jit(solution)/shard_map/cond/branch_49_fun/ppermute | solution.py:301
  99.2 0.0 all-to-all-done.1
  99.8 0.0 copy-done
  99.9 2.1 %shard_map.51 = (bf16[32,64,256]{2,1,0:T(8,128)(2,1)}, bf16[64,128]{1,0:T(8,128)(2,1)S(1)}) custom-call(s32[2,32]{1,0:T(2,128)S(1)} %get-tuple-element.887.table_ref, s32[1]{0:T(128)} %bitcast.5.many_ref, bf16[32,64,256]{2,1,0:T(8,128)(2,1)S(1)} %bitcast.16, bf16[64,256]{1,0:T(8,128)(2,1)S(1)} %get-tuple-element.892.left_ref, ...), custom_call_target="tpu_custom_call" | custom-call | tf_op jit(solution)/shard_map/pallas_call | solution.py:274
  101.9 6.5 %all-gather = bf16[128,128]{1,0:T(8,128)(2,1)S(1)} all-gather(bf16[64,128]{1,0:T(8,128)(2,1)S(1)} %get-tuple-element.896), channel_id=2, replica_groups=mesh['groups'=2,'seq'=16,'head'=8,'rep'=2] {'rep'}, dimensions={0}, use_global_device_ids=true | all-gather | bytes 49152 | tf_op jit(solution)/shard_map/all_gather | solution.py:341
  108.4 0.7 broadcast_select_fusion
  (5 shorter events, 0.0 us)
Async XLA Ops:
  4.6 94.7 %all-to-all-start.1 = ((bf16[16,2,64,256]{3,2,1,0:T(8,128)(2,1)}), bf16[16,2,64,256]{3,2,1,0:T(8,128)(2,1)S(1)}, u32[]{:S(2)}, u32[]{:S(2)}) async-start(bf16[16,2,64,256]{3,2,1,0:T(8,128)(2,1)} %bitcast.2), calls=%async_computation.1 | async-start | bytes 2097152 | tf_op jit(solution)/shard_map/all_to_all | solution.py:312
  49.4 50.4 %copy-start = (bf16[2,32,1,64,256]{4,3,2,1,0:T(8,128)(2,1)S(1)}, bf16[2,32,1,64,256]{4,3,2,1,0:T(8,128)(2,1)}, u32[]{:S(2)}) copy-start(bf16[2,32,1,64,256]{4,3,2,1,0:T(8,128)(2,1)} %cache_ref.1) | copy-start | bytes 6291460
  49.5 41.1 %collective-permute-start.87 = (bf16[64,256]{1,0:T(8,128)(2,1)S(1)}, bf16[64,256]{1,0:T(8,128)(2,1)S(1)}, u32[]{:S(2)}, u32[]{:S(2)}) collective-permute-start(bf16[64,256]{1,0:T(8,128)(2,1)S(1)} %get-tuple-element.691), channel_id=1, source_target_pairs={{0,64},{16,80},{32,96},{48,112},{64,128},{80,144},{96,160},{112,17... | collective-permute-start | bytes 98312 | tf_op jit(solution)/shard_map/cond/branch_49_fun/ppermute | solution.py:301
  56.7 42.5 %collective-permute-start.88 = (bf16[64,256]{1,0:T(8,128)(2,1)S(1)}, bf16[64,256]{1,0:T(8,128)(2,1)S(1)}, u32[]{:S(2)}, u32[]{:S(2)}) collective-permute-start(bf16[64,256]{1,0:T(8,128)(2,1)S(1)} %get-tuple-element.692), channel_id=1, source_target_pairs={{0,144},{16,160},{32,176},{48,192},{64,208},{80,224},{96,240},{112... | collective-permute-start | bytes 98312 | tf_op jit(solution)/shard_map/cond/branch_49_fun/ppermute | solution.py:301

commit v5 on v4

--- a/solution.py
+++ b/solution.py
@@ -212,7 +212,7 @@
 
 def place_kernel(
     table_ref, many_ref, base_ref, left_ref, right_ref, extra_ref,
-    out_ref, bounds_ref, spare, high, low, rows, sem, spare_sem,
+    out_ref, bounds_ref, spare, rows, sem, spare_sem,
 ):
     slots, head_width = base_ref.shape[0], base_ref.shape[-1] // 2
     pages = out_ref.shape[0]
@@ -232,25 +232,19 @@
             block = base_ref.at[jnp.minimum(t, slots - 1)]
             pltpu.make_async_copy(block, out_ref.at[i], sem).start()
 
-    def extremes(k, ref):
-        keys = ref[:, :head_width]
-        high[pl.ds(k, 1), :] = jnp.max(keys, axis=0, keepdims=True).astype(jnp.float32)
-        low[pl.ds(k, 1), :] = -jnp.min(keys, axis=0, keepdims=True).astype(jnp.float32)
-
-    for k in range(slots):
-        extremes(k, base_ref.at[k])
-    for k in range(3):
-        extremes(slots + k, spare.at[k])
-
     @pl.when(many_ref[0] != 0)
     def _():
         copy = pltpu.make_async_copy(extra_ref, spare.at[pl.ds(3, slots)], spare_sem)
         copy.start()
         copy.wait()
 
-        @pl.loop(0, slots)
-        def _(k):
-            extremes(slots + 3 + k, spare.at[3 + k])
+    for i in range(pages):
+        t = entry(i)
+        plain = base_ref[jnp.minimum(t, slots - 1), :, :head_width]
+        other = spare[jnp.maximum(t - slots, 0), :, :head_width]
+        keys = jnp.where(t < slots, plain, other)
+        rows[2 * i : 2 * i + 1, :] = jnp.max(keys, axis=0, keepdims=True).astype(jnp.float32)
+        rows[2 * i + 1 : 2 * i + 2, :] = -jnp.min(keys, axis=0, keepdims=True).astype(jnp.float32)
 
     for i in range(pages):
         t = entry(i)
@@ -259,9 +253,6 @@
         def _():
             block = spare.at[jnp.maximum(t - slots, 0)]
             pltpu.make_async_copy(block, out_ref.at[i], sem).start()
-
-        rows[pl.ds(2 * i, 1), :] = high[pl.ds(t, 1), :]
-        rows[pl.ds(2 * i + 1, 1), :] = low[pl.ds(t, 1), :]
 
     bounds_ref[...] = rows[...].astype(bounds_ref.dtype)
     pltpu.make_async_copy(out_ref, out_ref, sem).wait()
@@ -280,8 +271,6 @@
             out_specs=[hbm, vmem],
             scratch_shapes=[
                 pltpu.VMEM((3 + base.shape[0], *block), base.dtype),
-                pltpu.VMEM((3 + 2 * base.shape[0], head_width), jnp.float32),
-                pltpu.VMEM((3 + 2 * base.shape[0], head_width), jnp.float32),
                 pltpu.VMEM((2 * pages, head_width), jnp.float32),
                 pltpu.SemaphoreType.DMA,
                 pltpu.SemaphoreType.DMA,
@@ -332,7 +321,7 @@
         rounds, index, _ = lax.optimization_barrier(state)
         return rounds - 1, index, exchange(pack_seconds(index, kv_cache, slots))
 
-    base, payload, many = lax.optimization_barrier((base, payload, many))
+    base, payload = lax.optimization_barrier((base, payload))
     _, table, extra = lax.while_loop(lambda state: state[0] > 0, all_seconds, (many, table, payload))
 
     pages, half = place_pages(

time: 109 us -> 110 us (level)
  waiting for transfers between devices: 36.4 us -> 38.8 us
    ppermute x2, waiting for transfers between devices: 36.4 us -> 38.8 us  [swap(): lax.ppermute(block, 'seq', [(s, (s + shift) % size) for s in range(size)])]
  transfers between devices with their start and end apart: 3 -> 3, of which waited for: 2 -> 1; matrix products, arithmetic and copies ran while one was open for 0% -> 0% of each run, Pallas kernels for 0% -> 0%
where the time goes in v5:
time: 110 us
  starting transfers between devices  56.6 us (51%)
  waiting for transfers between devices  38.8 us (35%)
  Pallas kernels  6.02 us (5%)
  blocking collectives  5.77 us (5%)
  between operations  1.92 us (2%)
    all_to_all x1, starting transfers between devices, exchange(): lax.all_to_all(shaped, 'seq', split_axis=0, concat_axis=0, tiled=True)  44.2 us
    ppermute x2, waiting for transfers between devices, swap(): lax.ppermute(block, 'seq', [(s, (s + shift) % size) for s in range(size)])  38.8 us
    ppermute x2, starting transfers between devices, swap(): lax.ppermute(block, 'seq', [(s, (s + shift) % size) for s in range(size)])  12.4 us
    all_gather x1, blocking collectives, on_device(): halves = lax.all_gather(half, 'rep')  5.77 us
    pallas_call x1, Pallas kernels, plan_and_pack(): pl.pallas_call(functools.partial(plan_kernel, owners, cache.shape[1], pag...  3.92 us
  transfers between devices with their start and end apart: 3, of which 1 were waited for; matrix products, arithmetic and copies ran while one was open for 0% of the time, Pallas kernels for 0%

profile of v5, /device:TPU:65, one launch (start us, length us, event | category | flops | bytes accessed | tf_op | source)
XLA Modules:
  0.0 110.1 jit_solution(36051534873075582)
XLA Ops:
  0.6 3.9 %shard_map.50 = (bf16[32,64,256]{2,1,0:T(8,128)(2,1)}, bf16[64,256]{1,0:T(8,128)(2,1)S(1)}, bf16[64,256]{1,0:T(8,128)(2,1)S(1)}, s32[2,32]{1,0:T(2,128)S(1)}, s32[1]{0:T(128)}, /*index=5*/s32[1]{0:T(128)}) custom-call(s32[2,256]{1,0:T(2,128)} %keep_hbm.1, s32[2,256]{1,0:T(2,128)} %slot_hbm.1, bf16[2,32,1,64,256]{4,3,2,1,0:T(8,128)(2,1)} %cache_ref.1), custom_call_target="tpu_custom_call" | custom-call | tf_op jit(solution)/shard_map/pallas_call | solution.py:186
  4.6 44.2 %all-to-all-start.1 = ((bf16[16,2,64,256]{3,2,1,0:T(8,128)(2,1)}), bf16[16,2,64,256]{3,2,1,0:T(8,128)(2,1)S(1)}, u32[]{:S(2)}, u32[]{:S(2)}) async-start(bf16[16,2,64,256]{3,2,1,0:T(8,128)(2,1)} %bitcast.3), calls=%async_computation.1 | async-start | bytes 2097152 | tf_op jit(solution)/shard_map/all_to_all | solution.py:301
  50.0 0.0 copy-start
  50.0 51.5 %conditional.1 = ((bf16[64,256]{1,0:T(8,128)(2,1)S(1)}, bf16[64,256]{1,0:T(8,128)(2,1)S(1)})) conditional(s32[]{:T(128)} %bitcast.5, (bf16[64,256]{1,0:T(8,128)(2,1)S(1)}, bf16[64,256]{1,0:T(8,128)(2,1)S(1)}) %tuple.571, (bf16[64,256]{1,0:T(8,128)(2,1)S(1)}, bf16[64,256]{1,0:T(8,128)(2,1)S(1)}) %tuple.572, ...), branch_computations={%region_2.0_spmd, %region_3.0_spmd, %region_4.0_spmd, %region_5.0_... | conditional | bytes 393320 | solution.py:318
  50.3 8.9 %collective-permute-start.235 = (bf16[64,256]{1,0:T(8,128)(2,1)S(1)}, bf16[64,256]{1,0:T(8,128)(2,1)S(1)}, u32[]{:S(2)}, u32[]{:S(2)}) collective-permute-start(bf16[64,256]{1,0:T(8,128)(2,1)S(1)} %get-tuple-element.845), channel_id=1, source_target_pairs={{0,96},{16,112},{32,128},{48,144},{64,160},{80,176},{96,192},{112,... | collective-permute-start | bytes 98312 | tf_op jit(solution)/shard_map/cond/branch_126_fun/ppermute | solution.py:290
  59.3 3.4 %collective-permute-start.236 = (bf16[64,256]{1,0:T(8,128)(2,1)S(1)}, bf16[64,256]{1,0:T(8,128)(2,1)S(1)}, u32[]{:S(2)}, u32[]{:S(2)}) collective-permute-start(bf16[64,256]{1,0:T(8,128)(2,1)S(1)} %get-tuple-element.846), channel_id=1, source_target_pairs={{0,240},{16,0},{32,16},{48,32},{64,48},{80,64},{96,80},{112,96},{1... | collective-permute-start | bytes 98312 | tf_op jit(solution)/shard_map/cond/branch_126_fun/ppermute | solution.py:290
  62.7 38.8 %collective-permute-done.235 = bf16[64,256]{1,0:T(8,128)(2,1)S(1)} collective-permute-done((bf16[64,256]{1,0:T(8,128)(2,1)S(1)}, bf16[64,256]{1,0:T(8,128)(2,1)S(1)}, u32[]{:S(2)}, u32[]{:S(2)}) %collective-permute-start.235) | collective-permute-done | bytes 32800 | tf_op jit(solution)/shard_map/cond/branch_126_fun/ppermute | solution.py:290
  101.5 0.0 collective-permute-done.236
  101.5 0.0 all-to-all-done.1
  101.5 0.0 copy-done
  101.5 2.1 %shard_map.51 = (bf16[32,64,256]{2,1,0:T(8,128)(2,1)}, bf16[64,128]{1,0:T(8,128)(2,1)S(1)}) custom-call(s32[2,32]{1,0:T(2,128)S(1)} %get-tuple-element.885.table_ref, s32[1]{0:T(128)} %get-tuple-element.881.many_ref, bf16[32,64,256]{2,1,0:T(8,128)(2,1)S(1)} %bitcast.15, bf16[64,256]{1,0:T(8,128)(2,1)S(1)} %get-tuple-element.890.left_ref, ...), custom_call_target="tpu_custom_call" | custom-call | tf_op jit(solution)/shard_map/pallas_call | solution.py:265
  103.7 5.8 %all-gather = bf16[128,128]{1,0:T(8,128)(2,1)S(1)} all-gather(bf16[64,128]{1,0:T(8,128)(2,1)S(1)} %get-tuple-element.894), channel_id=2, replica_groups=mesh['groups'=2,'seq'=16,'head'=8,'rep'=2] {'rep'}, dimensions={0}, use_global_device_ids=true | all-gather | bytes 49152 | tf_op jit(solution)/shard_map/all_gather | solution.py:330
  109.4 0.7 broadcast_select_fusion
  (5 shorter events, 0.0 us)
Async XLA Ops:
  4.6 97.0 %all-to-all-start.1 = ((bf16[16,2,64,256]{3,2,1,0:T(8,128)(2,1)}), bf16[16,2,64,256]{3,2,1,0:T(8,128)(2,1)S(1)}, u32[]{:S(2)}, u32[]{:S(2)}) async-start(bf16[16,2,64,256]{3,2,1,0:T(8,128)(2,1)} %bitcast.3), calls=%async_computation.1 | async-start | bytes 2097152 | tf_op jit(solution)/shard_map/all_to_all | solution.py:301
  50.0 51.5 %copy-start = (bf16[2,32,1,64,256]{4,3,2,1,0:T(8,128)(2,1)S(1)}, bf16[2,32,1,64,256]{4,3,2,1,0:T(8,128)(2,1)}, u32[]{:S(2)}) copy-start(bf16[2,32,1,64,256]{4,3,2,1,0:T(8,128)(2,1)} %cache_ref.1) | copy-start | bytes 6291460
  50.3 51.2 %collective-permute-start.235 = (bf16[64,256]{1,0:T(8,128)(2,1)S(1)}, bf16[64,256]{1,0:T(8,128)(2,1)S(1)}, u32[]{:S(2)}, u32[]{:S(2)}) collective-permute-start(bf16[64,256]{1,0:T(8,128)(2,1)S(1)} %get-tuple-element.845), channel_id=1, source_target_pairs={{0,96},{16,112},{32,128},{48,144},{64,160},{80,176},{96,192},{112,... | collective-permute-start | bytes 98312 | tf_op jit(solution)/shard_map/cond/branch_126_fun/ppermute | solution.py:290
  59.3 42.2 %collective-permute-start.236 = (bf16[64,256]{1,0:T(8,128)(2,1)S(1)}, bf16[64,256]{1,0:T(8,128)(2,1)S(1)}, u32[]{:S(2)}, u32[]{:S(2)}) collective-permute-start(bf16[64,256]{1,0:T(8,128)(2,1)S(1)} %get-tuple-element.846), channel_id=1, source_target_pairs={{0,240},{16,0},{32,16},{48,32},{64,48},{80,64},{96,80},{112,96},{1... | collective-permute-start | bytes 98312 | tf_op jit(solution)/shard_map/cond/branch_126_fun/ppermute | solution.py:290
